TPU v7x, 512 devices: a whole 4x4x16 slice. The times are simulated.
512 devices in a mesh: gx: 16 (over z_lo, x), gy: 8 (over y, core), gz: 4 (over z_hi).
Axes of the slice: x: 4, y: 4, z: 16 (z_hi: 4, z_lo: 4; z = z_hi * 4 + z_lo), core: 2. Of those that a mesh axis runs over, the one named last changes fastest.
Arguments:
- populations: float32 [2, 19, 64, 128, 512], P(None, None, 'gx', 'gy', 'gz'), may hold values from 0.01 to 0.2
- solid: int32 [64, 128, 512], P('gx', 'gy', 'gz'), may hold values 0 or 1
Outputs:
- read: float32 [2, 19, 64, 128, 512], P(None, None, 'gx', 'gy', 'gz')
All inputs are finite; a program needn't handle non-finite values. No bound on the sum of `solid` on one device may be relied on, other than what follows from the above.
Results may differ from a plain program's by a relative error of at most 0.0001.
Values sent between devices are 32-bit elements; how exact they have to be, the bound alone decides.
A program may use at most 64 MiB of HBM per device.

v0:
```python
import jax
import jax.numpy as jnp
import numpy as np
from jax import lax
from jax.sharding import PartitionSpec as P

VELOCITIES = [
    (0, 0, 0),
    (1, 0, 0),
    (-1, 0, 0),
    (0, 1, 0),
    (0, -1, 0),
    (0, 0, 1),
    (0, 0, -1),
    (1, 1, 0),
    (-1, -1, 0),
    (1, -1, 0),
    (-1, 1, 0),
    (1, 0, 1),
    (-1, 0, -1),
    (1, 0, -1),
    (-1, 0, 1),
    (0, 1, 1),
    (0, -1, -1),
    (0, 1, -1),
    (0, -1, 1),
]
WEIGHTS = [1.0 / 3.0] + [1.0 / 18.0] * 6 + [1.0 / 36.0] * 12
OPPOSITE = [0, 2, 1, 4, 3, 6, 5, 8, 7, 10, 9, 12, 11, 14, 13, 16, 15, 18, 17]
coupling = 0.9
relax_times = (1.0, 0.8)
wall_values = (0.3, 1.5)


def extended(block, sides, width):
    for axis, dim in sides:
        count = lax.axis_size(axis)
        forward = [(i, i + 1) for i in range(count - 1)]
        forward.append((count - 1, 0))
        backward = [(target, source) for source, target in forward]
        low = lax.ppermute(
            lax.slice_in_dim(block, block.shape[dim] - width, None, axis=dim), axis, forward
        )
        high = lax.ppermute(lax.slice_in_dim(block, 0, width, axis=dim), axis, backward)
        block = jnp.concatenate([low, block, high], axis=dim)
    return block


def collide(populations, fluid, psi, gradient):
    vel = jnp.asarray(np.array(VELOCITIES, np.float32))
    weights = jnp.asarray(np.array(WEIGHTS, np.float32))
    rho = jnp.sum(populations, axis=1)
    moment = jnp.einsum("ia,kixyz->kaxyz", vel, populations, precision=lax.Precision.HIGHEST)
    inv_first = 1.0 / relax_times[0]
    inv_second = 1.0 / relax_times[1]
    weight_sum = rho[0] * inv_first + rho[1] * inv_second
    common = (moment[0] * inv_first + moment[1] * inv_second) / weight_sum[None]
    forces = (-coupling * psi[0][None] * gradient[1], -coupling * psi[1][None] * gradient[0])
    results = []
    for comp in range(2):
        velocity = common + relax_times[comp] * forces[comp] / rho[comp][None]
        along = jnp.einsum("ia,axyz->ixyz", vel, velocity, precision=lax.Precision.HIGHEST)
        speed_sq = jnp.sum(velocity * velocity, axis=0)
        equil = (
            weights[:, None, None, None]
            * rho[comp][None]
            * (1.0 + 3.0 * along + 4.5 * along * along - 1.5 * speed_sq[None])
        )
        current = populations[comp]
        results.append(current - (current - equil) / relax_times[comp])
    post = jnp.stack(results, axis=0)
    return jnp.where(fluid[None, None], post, populations)


def window(padded, offset, dim_first, sizes):
    out = padded
    for axis_idx in range(3):
        start = 1 + offset[axis_idx]
        out = lax.slice_in_dim(out, start, start + sizes[axis_idx], axis=dim_first + axis_idx)
    return out


def body(populations, solid):
    fluid = solid == 0
    sizes = solid.shape
    rho = jnp.sum(populations, axis=1)
    wall = jnp.asarray(np.array(wall_values, np.float32)).reshape(2, 1, 1, 1)
    psi = jnp.where(fluid[None], rho, wall)
    signed = jnp.where(fluid[None], psi, -psi)
    padded = extended(signed, (("gx", 1), ("gy", 2), ("gz", 3)), 1)
    psi_padded = jnp.abs(padded)
    fluid_padded = padded[0] > 0.0
    parts = [jnp.zeros_like(psi) for axis_idx in range(3)]
    for i in range(1, 19):
        move = VELOCITIES[i]
        beside = window(psi_padded, move, 1, sizes)
        for axis_idx in range(3):
            if move[axis_idx] != 0:
                parts[axis_idx] = parts[axis_idx] + WEIGHTS[i] * move[axis_idx] * beside
    gradient = jnp.stack(parts, axis=1)
    post = collide(populations, fluid, psi, gradient)
    halo_post = extended(post, (("gx", 2), ("gy", 3), ("gz", 4)), 1)
    pulled_all = jnp.stack(
        [
            window(
                halo_post[:, i], (-VELOCITIES[i][0], -VELOCITIES[i][1], -VELOCITIES[i][2]), 1, sizes
            )
            for i in range(19)
        ],
        axis=1,
    )
    moved = []
    for i in range(19):
        move = VELOCITIES[i]
        source_fluid = window(fluid_padded, (-move[0], -move[1], -move[2]), 0, sizes)
        moved.append(jnp.where(source_fluid[None], pulled_all[:, i], post[:, OPPOSITE[i]]))
    result = jnp.stack(moved, axis=1)
    return jnp.where(fluid[None, None], result, populations)


def solution(mesh):
    in_specs = (P(None, None, "gx", "gy", "gz"), P("gx", "gy", "gz"))
    out_specs = P(None, None, "gx", "gy", "gz")
    return jax.shard_map(body, mesh=mesh, in_specs=in_specs, out_specs=out_specs, check_vma=False)
```

profile of v0, /device:TPU:1, one launch (start us, length us, event | category | flops | bytes accessed | tf_op | source)
XLA Modules:
  0.0 123.8 jit_solution(9344121369777876025)
XLA Ops:
  0.0 0.9 broadcast_compare_fusion
  0.9 1.4 %reduce_sum.27 = f32[2,4,16,128]{3,2,1,0:T(8,128)S(1)} reduce(f32[2,19,4,16,128]{4,3,2,1,0:T(8,128)} %param.5, f32[]{:T(128)} %constant.17.clone.1), dimensions={1}, to_apply=%region_0.0 | reduce | flops 294912 | bytes 1310724 | tf_op jit(solution)/shard_map/reduce_sum | solution.py:86
  2.4 3.9 %collective-permute-start = (f32[2,1,16,128]{3,2,1,0:T(8,128)S(1)}, f32[2,1,16,128]{3,2,1,0:T(8,128)S(1)}, u32[]{:S(2)}, u32[]{:S(2)}) collective-permute-start(f32[2,1,16,128]{3,2,1,0:T(8,128)S(1)} %get-tuple-element.49), channel_id=1, source_target_pairs={{0,32},{32,64},{64,96},{96,128},{128,160},{160,192},{192,224},{224... | collective-permute-start | bytes 49160 | tf_op jit(solution)/shard_map/ppermute | solution.py:41
  6.3 7.2 %collective-permute-start.1 = (f32[2,1,16,128]{3,2,1,0:T(8,128)S(1)}, f32[2,1,16,128]{3,2,1,0:T(8,128)S(1)}, u32[]{:S(2)}, u32[]{:S(2)}) collective-permute-start(f32[2,1,16,128]{3,2,1,0:T(8,128)S(1)} %get-tuple-element.50), channel_id=1, source_target_pairs={{32,0},{64,32},{96,64},{128,96},{160,128},{192,160},{224,192},{256... | collective-permute-start | bytes 49160 | tf_op jit(solution)/shard_map/ppermute | solution.py:44
  13.6 1.6 %convolution_bitcast_fusion = f32[2,3,4,16,128]{4,1,3,2,0:T(4,128)S(1)} fusion(f32[19,3,1,1,1]{0,1,4,3,2:T(4,128)S(1)} %copy-done.22, f32[2,19,4,16,128]{4,3,2,1,0:T(8,128)S(1)} %copy-done), kind=kOutput, calls=%fused_computation.7 | convolution fusion | flops 11206656 | bytes 1442020 | tf_op jit(solution)/shard_map/ia,kixyz->kaxyz/dot_general | solution.py:53
  15.2 2.1 %collective-permute-start.2 = (f32[2,6,1,128]{3,2,1,0:T(1,128)S(1)}, f32[2,6,1,128]{3,2,1,0:T(1,128)S(1)}, u32[]{:S(2)}, u32[]{:S(2)}) collective-permute-start(f32[2,6,1,128]{3,2,1,0:T(1,128)S(1)} %get-tuple-element.40), channel_id=1, source_target_pairs={{0,4},{4,8},{8,12},{12,16},{16,20},{20,24},{24,28},{28,0},{1,5},{5... | collective-permute-start | bytes 18440 | tf_op jit(solution)/shard_map/ppermute | solution.py:41
  17.4 3.3 %collective-permute-start.3 = (f32[2,6,1,128]{3,2,1,0:T(1,128)S(1)}, f32[2,6,1,128]{3,2,1,0:T(1,128)S(1)}, u32[]{:S(2)}, u32[]{:S(2)}) collective-permute-start(f32[2,6,1,128]{3,2,1,0:T(1,128)S(1)} %get-tuple-element.41), channel_id=1, source_target_pairs={{4,0},{8,4},{12,8},{16,12},{20,16},{24,20},{28,24},{0,28},{5,1},{9... | collective-permute-start | bytes 18440 | tf_op jit(solution)/shard_map/ppermute | solution.py:44
  21.6 7.8 %collective-permute-start.4 = (f32[2,6,18,1]{3,2,1,0:T(8,128)S(1)}, f32[2,6,18,1]{3,2,1,0:T(8,128)S(1)}, u32[]{:S(2)}, u32[]{:S(2)}) collective-permute-start(f32[2,6,18,1]{3,2,1,0:T(8,128)S(1)} %get-tuple-element.38), channel_id=1, source_target_pairs={{0,1},{1,2},{2,3},{3,0},{4,5},{5,6},{6,7},{7,4},{8,9},{9,10},{10,1... | collective-permute-start | bytes 2600 | tf_op jit(solution)/shard_map/ppermute | solution.py:41
  29.4 4.7 %collective-permute-start.5 = (f32[2,6,18,1]{3,2,1,0:T(8,128)S(1)}, f32[2,6,18,1]{3,2,1,0:T(8,128)S(1)}, u32[]{:S(2)}, u32[]{:S(2)}) collective-permute-start(f32[2,6,18,1]{3,2,1,0:T(8,128)S(1)} %get-tuple-element.39), channel_id=1, source_target_pairs={{1,0},{2,1},{3,2},{0,3},{5,4},{6,5},{7,6},{4,7},{9,8},{10,9},{11,1... | collective-permute-start | bytes 2600 | tf_op jit(solution)/shard_map/ppermute | solution.py:44
  34.1 0.7 copy.36
  34.8 9.3 %collective-permute-done.4 = f32[2,6,18,1]{3,2,1,0:T(8,128)S(1)} collective-permute-done((f32[2,6,18,1]{3,2,1,0:T(8,128)S(1)}, f32[2,6,18,1]{3,2,1,0:T(8,128)S(1)}, u32[]{:S(2)}, u32[]{:S(2)}) %collective-permute-start.4) | collective-permute-done | bytes 896 | tf_op jit(solution)/shard_map/ppermute | solution.py:41
  44.1 5.7 %collective-permute-done.5 = f32[2,6,18,1]{3,2,1,0:T(8,128)S(1)} collective-permute-done((f32[2,6,18,1]{3,2,1,0:T(8,128)S(1)}, f32[2,6,18,1]{3,2,1,0:T(8,128)S(1)}, u32[]{:S(2)}, u32[]{:S(2)}) %collective-permute-start.5) | collective-permute-done | bytes 896 | tf_op jit(solution)/shard_map/ppermute | solution.py:44
  51.2 1.1 fusion.10
  52.3 1.1 fusion.3
  53.4 0.9 maximum_select_fusion
  54.6 1.9 %collective-permute-start.6 = (f32[2,19,1,16,128]{4,3,2,0,1:T(8,128)S(1)}, f32[2,19,1,16,128]{4,3,2,0,1:T(8,128)S(1)}, u32[]{:S(2)}, u32[]{:S(2)}) collective-permute-start(f32[2,19,1,16,128]{4,3,2,0,1:T(8,128)S(1)} %get-tuple-element.35), channel_id=1, source_target_pairs={{0,32},{32,64},{64,96},{96,128},{128,160},{160,192},{192,224},{224... | collective-permute-start | bytes 933896 | tf_op jit(solution)/shard_map/ppermute | solution.py:41
  56.5 8.5 %collective-permute-start.7 = (f32[2,19,1,16,128]{4,3,2,0,1:T(8,128)S(1)}, f32[2,19,1,16,128]{4,3,2,0,1:T(8,128)S(1)}, u32[]{:S(2)}, u32[]{:S(2)}) collective-permute-start(f32[2,19,1,16,128]{4,3,2,0,1:T(8,128)S(1)} %get-tuple-element.34), channel_id=1, source_target_pairs={{32,0},{64,32},{96,64},{128,96},{160,128},{192,160},{224,192},{256... | collective-permute-start | bytes 933896 | tf_op jit(solution)/shard_map/ppermute | solution.py:44
  65.0 4.9 %collective-permute-done.6 = f32[2,19,1,16,128]{4,3,2,0,1:T(8,128)S(1)} collective-permute-done((f32[2,19,1,16,128]{4,3,2,0,1:T(8,128)S(1)}, f32[2,19,1,16,128]{4,3,2,0,1:T(8,128)S(1)}, u32[]{:S(2)}, u32[]{:S(2)}) %collective-permute-start.6) | collective-permute-done | bytes 311328 | tf_op jit(solution)/shard_map/ppermute | solution.py:41
  71.0 2.5 %collective-permute-start.8 = (f32[2,19,6,1,128]{4,3,2,0,1:T(1,128)S(1)}, f32[2,19,6,1,128]{4,3,2,0,1:T(1,128)S(1)}, u32[]{:S(2)}, u32[]{:S(2)}) collective-permute-start(f32[2,19,6,1,128]{4,3,2,0,1:T(1,128)S(1)} %get-tuple-element.32), channel_id=1, source_target_pairs={{0,4},{4,8},{8,12},{12,16},{16,20},{20,24},{24,28},{28,0},{1,5},{5... | collective-permute-start | bytes 350216 | tf_op jit(solution)/shard_map/ppermute | solution.py:41
  73.5 1.8 %collective-permute-done.8 = f32[2,19,6,1,128]{4,3,2,0,1:T(1,128)S(1)} collective-permute-done((f32[2,19,6,1,128]{4,3,2,0,1:T(1,128)S(1)}, f32[2,19,6,1,128]{4,3,2,0,1:T(1,128)S(1)}, u32[]{:S(2)}, u32[]{:S(2)}) %collective-permute-start.8) | collective-permute-done | bytes 116768 | tf_op jit(solution)/shard_map/ppermute | solution.py:41
  75.3 2.5 %collective-permute-done.9 = f32[2,19,6,1,128]{4,3,2,0,1:T(1,128)S(1)} collective-permute-done((f32[2,19,6,1,128]{4,3,2,0,1:T(1,128)S(1)}, f32[2,19,6,1,128]{4,3,2,0,1:T(1,128)S(1)}, u32[]{:S(2)}, u32[]{:S(2)}) %collective-permute-start.9) | collective-permute-done | bytes 116768 | tf_op jit(solution)/shard_map/ppermute | solution.py:44
  78.3 3.4 %fusion.105 = (f32[2,19,6,18,1]{4,3,2,0,1:T(8,128)}, f32[2,19,6,18,1]{4,3,2,0,1:T(8,128)}) fusion(f32[2,19,6,18,128]{4,3,2,0,1:T(8,128)S(1)} %pad_maximum_fusion.1), kind=kLoop, calls=%fused_computation.192 | loop fusion | bytes 65664 | tf_op jit(solution)/shard_map/slice | solution.py:42
  81.7 2.9 %copy.46 = f32[2,19,6,18,1]{1,0,4,3,2:T(2,128)S(1)} copy(f32[2,19,6,18,1]{4,3,2,0,1:T(8,128)} %get-tuple-element.30) | data formatting | bytes 32832 | tf_op jit(solution)/shard_map/slice | solution.py:42
  84.6 2.9 %copy.47 = f32[2,19,6,18,1]{1,0,4,3,2:T(2,128)S(1)} copy(f32[2,19,6,18,1]{4,3,2,0,1:T(8,128)} %get-tuple-element.31) | data formatting | bytes 32832 | tf_op jit(solution)/shard_map/slice | solution.py:44
  87.5 3.4 %collective-permute-start.11 = (f32[2,19,6,18,1]{1,0,4,3,2:T(2,128)S(1)}, f32[2,19,6,18,1]{1,0,4,3,2:T(2,128)}, u32[]{:S(2)}, u32[]{:S(2)}) collective-permute-start(f32[2,19,6,18,1]{1,0,4,3,2:T(2,128)S(1)} %copy.47), channel_id=1, source_target_pairs={{1,0},{2,1},{3,2},{0,3},{5,4},{6,5},{7,6},{4,7},{9,8},{10,9},{11,1... | collective-permute-start | bytes 49256 | tf_op jit(solution)/shard_map/ppermute | solution.py:44
  90.9 6.0 %collective-permute-start.10 = (f32[2,19,6,18,1]{1,0,4,3,2:T(2,128)S(1)}, f32[2,19,6,18,1]{1,0,4,3,2:T(2,128)S(1)}, u32[]{:S(2)}, u32[]{:S(2)}) collective-permute-start(f32[2,19,6,18,1]{1,0,4,3,2:T(2,128)S(1)} %copy.46), channel_id=1, source_target_pairs={{0,1},{1,2},{2,3},{3,0},{4,5},{5,6},{6,7},{7,4},{8,9},{9,10},{10,1... | collective-permute-start | bytes 49256 | tf_op jit(solution)/shard_map/ppermute | solution.py:41
  96.9 0.8 fusion.110
  97.8 8.4 %collective-permute-done.10 = f32[2,19,6,18,1]{1,0,4,3,2:T(2,128)S(1)} collective-permute-done((f32[2,19,6,18,1]{1,0,4,3,2:T(2,128)S(1)}, f32[2,19,6,18,1]{1,0,4,3,2:T(2,128)S(1)}, u32[]{:S(2)}, u32[]{:S(2)}) %collective-permute-start.10) | collective-permute-done | bytes 16448 | tf_op jit(solution)/shard_map/ppermute | solution.py:41
  106.2 3.2 %copy.48 = f32[2,19,6,18,1]{4,3,2,0,1:T(8,128)} copy(f32[2,19,6,18,1]{1,0,4,3,2:T(2,128)S(1)} %collective-permute-done.10) | data formatting | bytes 32832 | tf_op jit(solution)/shard_map/ppermute | solution.py:41
  109.5 4.1 %copy.49 = f32[2,19,6,18,1]{4,3,2,0,1:T(8,128)} copy(f32[2,19,6,18,1]{1,0,4,3,2:T(2,128)} %collective-permute-done.11) | data formatting | bytes 32832 | tf_op jit(solution)/shard_map/ppermute | solution.py:44
  113.6 6.0 %pad_maximum_fusion = f32[2,19,6,18,130]{4,3,2,0,1:T(8,128)S(1)} fusion(f32[2,19,6,18,1]{4,3,2,0,1:T(8,128)} %copy.49, f32[2,19,6,1,128]{4,3,2,0,1:T(1,128)S(1)} %collective-permute-done.9, f32[2,19,6,16,128]{4,3,2,0,1:T(8,128)S(1)} %copy-done.2, f32[2,19,6,1,128]{4,3,2,0,1:T(1,128)S(1)} %collective-permute-done.8, f32[2,19,6,18,1]{4,3,2,0,1:T(8,128)} %copy.48), kind=kLoop, calls=%fused_computation | loop fusion | flops 2134080 | bytes 4268160 | tf_op jit(solution)/shard_map/concatenate | solution.py:45
  122.7 1.1 copy.69
  (103 shorter events, 7.0 us)
Async XLA Ops:
  0.0 2.3 %copy-start.23 = (f32[2]{0:T(128)S(1)}, f32[2]{0:T(128)}, u32[]{:S(2)}) copy-start(f32[2]{0:T(128)} %constant.14.clone) | copy-start | bytes 28
  0.0 13.6 %copy-start.22 = (f32[19,3,1,1,1]{0,1,4,3,2:T(4,128)S(1)}, f32[19,3,1,1,1]{0,1,4,3,2:T(4,128)}, u32[]{:S(2)}) copy-start(f32[19,3,1,1,1]{0,1,4,3,2:T(4,128)} %constant.42) | copy-start | bytes 688
  0.0 13.6 %copy-start = (f32[2,19,4,16,128]{4,3,2,1,0:T(8,128)S(1)}, f32[2,19,4,16,128]{4,3,2,1,0:T(8,128)}, u32[]{:S(2)}) copy-start(f32[2,19,4,16,128]{4,3,2,1,0:T(8,128)} %param.5) | copy-start | bytes 3735556
  2.4 12.8 %collective-permute-start = (f32[2,1,16,128]{3,2,1,0:T(8,128)S(1)}, f32[2,1,16,128]{3,2,1,0:T(8,128)S(1)}, u32[]{:S(2)}, u32[]{:S(2)}) collective-permute-start(f32[2,1,16,128]{3,2,1,0:T(8,128)S(1)} %get-tuple-element.49), channel_id=1, source_target_pairs={{0,32},{32,64},{64,96},{96,128},{128,160},{160,192},{192,224},{224... | collective-permute-start | bytes 49160 | tf_op jit(solution)/shard_map/ppermute | solution.py:41
  6.3 8.9 %collective-permute-start.1 = (f32[2,1,16,128]{3,2,1,0:T(8,128)S(1)}, f32[2,1,16,128]{3,2,1,0:T(8,128)S(1)}, u32[]{:S(2)}, u32[]{:S(2)}) collective-permute-start(f32[2,1,16,128]{3,2,1,0:T(8,128)S(1)} %get-tuple-element.50), channel_id=1, source_target_pairs={{32,0},{64,32},{96,64},{128,96},{160,128},{192,160},{224,192},{256... | collective-permute-start | bytes 49160 | tf_op jit(solution)/shard_map/ppermute | solution.py:44
  15.2 6.1 %collective-permute-start.2 = (f32[2,6,1,128]{3,2,1,0:T(1,128)S(1)}, f32[2,6,1,128]{3,2,1,0:T(1,128)S(1)}, u32[]{:S(2)}, u32[]{:S(2)}) collective-permute-start(f32[2,6,1,128]{3,2,1,0:T(1,128)S(1)} %get-tuple-element.40), channel_id=1, source_target_pairs={{0,4},{4,8},{8,12},{12,16},{16,20},{20,24},{24,28},{28,0},{1,5},{5... | collective-permute-start | bytes 18440 | tf_op jit(solution)/shard_map/ppermute | solution.py:41
  17.4 4.1 %collective-permute-start.3 = (f32[2,6,1,128]{3,2,1,0:T(1,128)S(1)}, f32[2,6,1,128]{3,2,1,0:T(1,128)S(1)}, u32[]{:S(2)}, u32[]{:S(2)}) collective-permute-start(f32[2,6,1,128]{3,2,1,0:T(1,128)S(1)} %get-tuple-element.41), channel_id=1, source_target_pairs={{4,0},{8,4},{12,8},{16,12},{20,16},{24,20},{28,24},{0,28},{5,1},{9... | collective-permute-start | bytes 18440 | tf_op jit(solution)/shard_map/ppermute | solution.py:44
  21.6 22.5 %collective-permute-start.4 = (f32[2,6,18,1]{3,2,1,0:T(8,128)S(1)}, f32[2,6,18,1]{3,2,1,0:T(8,128)S(1)}, u32[]{:S(2)}, u32[]{:S(2)}) collective-permute-start(f32[2,6,18,1]{3,2,1,0:T(8,128)S(1)} %get-tuple-element.38), channel_id=1, source_target_pairs={{0,1},{1,2},{2,3},{3,0},{4,5},{5,6},{6,7},{7,4},{8,9},{9,10},{10,1... | collective-permute-start | bytes 2600 | tf_op jit(solution)/shard_map/ppermute | solution.py:41
  29.4 20.4 %collective-permute-start.5 = (f32[2,6,18,1]{3,2,1,0:T(8,128)S(1)}, f32[2,6,18,1]{3,2,1,0:T(8,128)S(1)}, u32[]{:S(2)}, u32[]{:S(2)}) collective-permute-start(f32[2,6,18,1]{3,2,1,0:T(8,128)S(1)} %get-tuple-element.39), channel_id=1, source_target_pairs={{1,0},{2,1},{3,2},{0,3},{5,4},{6,5},{7,6},{4,7},{9,8},{10,9},{11,1... | collective-permute-start | bytes 2600 | tf_op jit(solution)/shard_map/ppermute | solution.py:44
  54.5 15.6 %copy-start.3 = (f32[2,19,4,16,128]{4,3,2,0,1:T(8,128)}, f32[2,19,4,16,128]{4,3,2,0,1:T(8,128)S(1)}, u32[]{:S(2)}) copy-start(f32[2,19,4,16,128]{4,3,2,0,1:T(8,128)S(1)} %copy.43) | copy-start | bytes 3735556
  54.6 15.3 %collective-permute-start.6 = (f32[2,19,1,16,128]{4,3,2,0,1:T(8,128)S(1)}, f32[2,19,1,16,128]{4,3,2,0,1:T(8,128)S(1)}, u32[]{:S(2)}, u32[]{:S(2)}) collective-permute-start(f32[2,19,1,16,128]{4,3,2,0,1:T(8,128)S(1)} %get-tuple-element.35), channel_id=1, source_target_pairs={{0,32},{32,64},{64,96},{96,128},{128,160},{160,192},{192,224},{224... | collective-permute-start | bytes 933896 | tf_op jit(solution)/shard_map/ppermute | solution.py:41
  56.5 14.2 %collective-permute-start.7 = (f32[2,19,1,16,128]{4,3,2,0,1:T(8,128)S(1)}, f32[2,19,1,16,128]{4,3,2,0,1:T(8,128)S(1)}, u32[]{:S(2)}, u32[]{:S(2)}) collective-permute-start(f32[2,19,1,16,128]{4,3,2,0,1:T(8,128)S(1)} %get-tuple-element.34), channel_id=1, source_target_pairs={{32,0},{64,32},{96,64},{128,96},{160,128},{192,160},{224,192},{256... | collective-permute-start | bytes 933896 | tf_op jit(solution)/shard_map/ppermute | solution.py:44
  70.8 7.0 %copy-start.1 = (f32[2,19,6,16,128]{4,3,2,0,1:T(8,128)}, f32[2,19,6,16,128]{4,3,2,0,1:T(8,128)S(1)}, u32[]{:S(2)}) copy-start(f32[2,19,6,16,128]{4,3,2,0,1:T(8,128)S(1)} %constant_dynamic-update-slice_fusion) | copy-start | bytes 5603332
  71.0 4.3 %collective-permute-start.8 = (f32[2,19,6,1,128]{4,3,2,0,1:T(1,128)S(1)}, f32[2,19,6,1,128]{4,3,2,0,1:T(1,128)S(1)}, u32[]{:S(2)}, u32[]{:S(2)}) collective-permute-start(f32[2,19,6,1,128]{4,3,2,0,1:T(1,128)S(1)} %get-tuple-element.32), channel_id=1, source_target_pairs={{0,4},{4,8},{8,12},{12,16},{16,20},{20,24},{24,28},{28,0},{1,5},{5... | collective-permute-start | bytes 350216 | tf_op jit(solution)/shard_map/ppermute | solution.py:41
  73.5 4.4 %collective-permute-start.9 = (f32[2,19,6,1,128]{4,3,2,0,1:T(1,128)S(1)}, f32[2,19,6,1,128]{4,3,2,0,1:T(1,128)S(1)}, u32[]{:S(2)}, u32[]{:S(2)}) collective-permute-start(f32[2,19,6,1,128]{4,3,2,0,1:T(1,128)S(1)} %get-tuple-element.33), channel_id=1, source_target_pairs={{4,0},{8,4},{12,8},{16,12},{20,16},{24,20},{28,24},{0,28},{5,1},{9... | collective-permute-start | bytes 350216 | tf_op jit(solution)/shard_map/ppermute | solution.py:44
  87.5 22.0 %collective-permute-start.11 = (f32[2,19,6,18,1]{1,0,4,3,2:T(2,128)S(1)}, f32[2,19,6,18,1]{1,0,4,3,2:T(2,128)}, u32[]{:S(2)}, u32[]{:S(2)}) collective-permute-start(f32[2,19,6,18,1]{1,0,4,3,2:T(2,128)S(1)} %copy.47), channel_id=1, source_target_pairs={{1,0},{2,1},{3,2},{0,3},{5,4},{6,5},{7,6},{4,7},{9,8},{10,9},{11,1... | collective-permute-start | bytes 49256 | tf_op jit(solution)/shard_map/ppermute | solution.py:44
  90.9 15.3 %collective-permute-start.10 = (f32[2,19,6,18,1]{1,0,4,3,2:T(2,128)S(1)}, f32[2,19,6,18,1]{1,0,4,3,2:T(2,128)S(1)}, u32[]{:S(2)}, u32[]{:S(2)}) collective-permute-start(f32[2,19,6,18,1]{1,0,4,3,2:T(2,128)S(1)} %copy.46), channel_id=1, source_target_pairs={{0,1},{1,2},{2,3},{3,0},{4,5},{5,6},{6,7},{7,4},{8,9},{9,10},{10,1... | collective-permute-start | bytes 49256 | tf_op jit(solution)/shard_map/ppermute | solution.py:41
  109.5 4.2 %copy-start.2 = (f32[2,19,6,16,128]{4,3,2,0,1:T(8,128)S(1)}, f32[2,19,6,16,128]{4,3,2,0,1:T(8,128)}, u32[]{:S(2)}) copy-start(f32[2,19,6,16,128]{4,3,2,0,1:T(8,128)} %copy-done.1) | copy-start | bytes 5603332
  119.6 1.3 %copy-start.4 = (f32[2,19,4,16,128]{4,3,2,0,1:T(8,128)S(1)}, f32[2,19,4,16,128]{4,3,2,0,1:T(8,128)}, u32[]{:S(2)}) copy-start(f32[2,19,4,16,128]{4,3,2,0,1:T(8,128)} %copy-done.3) | copy-start | bytes 3735556
  119.6 1.3 %copy-start.21 = (pred[4,16,128]{2,1,0:T(8,128)(4,1)S(1)}, pred[4,16,128]{2,1,0:T(8,128)(4,1)}, u32[]{:S(2)}) copy-start(pred[4,16,128]{2,1,0:T(8,128)(4,1)} %get-tuple-element.69) | copy-start | bytes 24580
  119.6 1.4 %copy-start.20 = (pred[4,16,128]{2,1,0:T(8,128)(4,1)S(1)}, pred[4,16,128]{2,1,0:T(8,128)(4,1)}, u32[]{:S(2)}) copy-start(pred[4,16,128]{2,1,0:T(8,128)(4,1)} %get-tuple-element.68) | copy-start | bytes 24580
  119.6 1.5 %copy-start.19 = (pred[4,16,128]{2,1,0:T(8,128)(4,1)S(1)}, pred[4,16,128]{2,1,0:T(8,128)(4,1)}, u32[]{:S(2)}) copy-start(pred[4,16,128]{2,1,0:T(8,128)(4,1)} %get-tuple-element.67) | copy-start | bytes 24580
  119.6 1.6 %copy-start.18 = (pred[4,16,128]{2,1,0:T(8,128)(4,1)S(1)}, pred[4,16,128]{2,1,0:T(8,128)(4,1)}, u32[]{:S(2)}) copy-start(pred[4,16,128]{2,1,0:T(8,128)(4,1)} %get-tuple-element.66) | copy-start | bytes 24580
  119.7 1.7 %copy-start.17 = (pred[4,16,128]{2,1,0:T(8,128)(4,1)S(1)}, pred[4,16,128]{2,1,0:T(8,128)(4,1)}, u32[]{:S(2)}) copy-start(pred[4,16,128]{2,1,0:T(8,128)(4,1)} %get-tuple-element.65) | copy-start | bytes 24580
  119.7 1.8 %copy-start.16 = (pred[4,16,128]{2,1,0:T(8,128)(4,1)S(1)}, pred[4,16,128]{2,1,0:T(8,128)(4,1)}, u32[]{:S(2)}) copy-start(pred[4,16,128]{2,1,0:T(8,128)(4,1)} %get-tuple-element.64) | copy-start | bytes 24580
  120.3 1.2 copy-start.15
  120.3 1.3 %copy-start.14 = (pred[4,16,128]{2,1,0:T(8,128)(4,1)S(1)}, pred[4,16,128]{2,1,0:T(8,128)(4,1)}, u32[]{:S(2)}) copy-start(pred[4,16,128]{2,1,0:T(8,128)(4,1)} %get-tuple-element.62) | copy-start | bytes 24580
  120.3 1.4 %copy-start.13 = (pred[4,16,128]{2,1,0:T(8,128)(4,1)S(1)}, pred[4,16,128]{2,1,0:T(8,128)(4,1)}, u32[]{:S(2)}) copy-start(pred[4,16,128]{2,1,0:T(8,128)(4,1)} %get-tuple-element.61) | copy-start | bytes 24580
  120.3 1.5 %copy-start.12 = (pred[4,16,128]{2,1,0:T(8,128)(4,1)S(1)}, pred[4,16,128]{2,1,0:T(8,128)(4,1)}, u32[]{:S(2)}) copy-start(pred[4,16,128]{2,1,0:T(8,128)(4,1)} %get-tuple-element.60) | copy-start | bytes 24580
  120.3 1.6 %copy-start.11 = (pred[4,16,128]{2,1,0:T(8,128)(4,1)S(1)}, pred[4,16,128]{2,1,0:T(8,128)(4,1)}, u32[]{:S(2)}) copy-start(pred[4,16,128]{2,1,0:T(8,128)(4,1)} %get-tuple-element.59) | copy-start | bytes 24580
  120.3 1.7 %copy-start.10 = (pred[4,16,128]{2,1,0:T(8,128)(4,1)S(1)}, pred[4,16,128]{2,1,0:T(8,128)(4,1)}, u32[]{:S(2)}) copy-start(pred[4,16,128]{2,1,0:T(8,128)(4,1)} %get-tuple-element.58) | copy-start | bytes 24580
  121.0 1.1 copy-start.8
  (6 other events, 5.6 us)
where the time goes:
time: 124 us
  starting transfers between devices  51.3 us (41%)
  waiting for transfers between devices  34.1 us (28%)
  local copies, waits for them, and re-layouts  21.4 us (17%)
  other arithmetic  12.5 us (10%)
  matrix products  3.77 us (3%)
    ppermute x6, starting transfers between devices, extended(): lax.ppermute(lax.slice_in_dim(block, 0, width, axis=dim), axis, backward)  27.1 us
    ppermute x6, waiting for transfers between devices, extended(): lax.ppermute(lax.slice_in_dim(block, block.shape[dim] - width, None, axis...  25.1 us
    ppermute x6, starting transfers between devices, extended(): lax.ppermute(lax.slice_in_dim(block, block.shape[dim] - width, None, axis...  24.2 us
    ppermute x6, waiting for transfers between devices, extended(): lax.ppermute(lax.slice_in_dim(block, 0, width, axis=dim), axis, backward)  9.08 us
    slice x5, local copies, waits for them, and re-layouts, extended(): lax.slice_in_dim(block, block.shape[dim] - width, None, axis=dim)  6.56 us
    concatenate x3, other arithmetic, extended(): block = jnp.concatenate([low, block, high], axis=dim)  6.5 us
    ppermute x1, local copies, waits for them, and re-layouts, extended(): lax.ppermute(lax.slice_in_dim(block, 0, width, axis=dim), axis, backward)  4.15 us
    ppermute x1, local copies, waits for them, and re-layouts, extended(): lax.ppermute(lax.slice_in_dim(block, block.shape[dim] - width, None, axis...  3.21 us
  transfers between devices with their start and end apart: 12, of which 9 were waited for; matrix products, arithmetic and copies ran while one was open for 5% of the time, Pallas kernels for 0%

commit v1 on v0

v1 whole, which is shorter than its diff:
```python
import functools

import jax
import jax.numpy as jnp
from jax import lax
from jax.experimental import pallas as pl
from jax.experimental.pallas import tpu as pltpu
from jax.sharding import PartitionSpec as P

VELOCITIES = [
    (0, 0, 0),
    (1, 0, 0),
    (-1, 0, 0),
    (0, 1, 0),
    (0, -1, 0),
    (0, 0, 1),
    (0, 0, -1),
    (1, 1, 0),
    (-1, -1, 0),
    (1, -1, 0),
    (-1, 1, 0),
    (1, 0, 1),
    (-1, 0, -1),
    (1, 0, -1),
    (-1, 0, 1),
    (0, 1, 1),
    (0, -1, -1),
    (0, 1, -1),
    (0, -1, 1),
]
WEIGHTS = [1.0 / 3.0] + [1.0 / 18.0] * 6 + [1.0 / 36.0] * 12
OPPOSITE = [0, 2, 1, 4, 3, 6, 5, 8, 7, 10, 9, 12, 11, 14, 13, 16, 15, 18, 17]
PAIRS = [(1, 2), (3, 4), (5, 6), (7, 8), (9, 10), (11, 12), (13, 14), (15, 16), (17, 18)]
coupling = 0.9
relax_times = (1.0, 0.8)
wall_values = (0.3, 1.5)

NX_L, NY_L, NZ_L = 4, 16, 128
ROWS = 24
X_DIRS = ([i for i in range(19) if VELOCITIES[i][0] == 1], [i for i in range(19) if VELOCITIES[i][0] == -1])
Y_DIRS = ([i for i in range(19) if VELOCITIES[i][1] == 1], [i for i in range(19) if VELOCITIES[i][1] == -1])
Z_LOW = [i for i in range(19) if VELOCITIES[i][2] == 1]
Z_HIGH = [OPPOSITE[i] for i in Z_LOW]
BIG = 1e30
LIMIT = 1e28
FACE, DIAG = 1.0 / 18.0, 1.0 / 36.0
MESH = pl.DeviceIdType.MESH


def roll(a, shift, axis):
    return pltpu.roll(a, shift % a.shape[axis], axis)


def posts(k, fluid, rho, v, dirs, old):
    scale = 1.0 / relax_times[k]
    r = jnp.where(fluid, rho * scale, 0.0)
    b = [1.5 * c for c in v]
    quad = b[0] * b[0] + b[1] * b[1] + b[2] * b[2]
    base = r - (2.0 / 3.0) * r * quad
    base = jnp.where(fluid, base, BIG)
    out = {}

    def keep(i, eq):
        out[i] = eq if k == 0 else eq + (1.0 - scale) * old(i)

    if 0 in dirs:
        keep(0, WEIGHTS[0] * base)
    by_weight = {}
    for pair in PAIRS:
        if not any(i in dirs for i in pair):
            continue
        i = pair[0]
        w = WEIGHTS[i]
        if w not in by_weight:
            by_weight[w] = (w * base, (2.0 * w) * r)
        wb, wr = by_weight[w]
        along = None
        for axis in range(3):
            c = VELOCITIES[i][axis]
            if c:
                along = (b[axis] if c > 0 else -b[axis]) if along is None else (along + b[axis] if c > 0 else along - b[axis])
        t = wr * along
        s = wb + along * t
        if i in dirs:
            keep(i, s + t)
        if pair[1] in dirs:
            keep(pair[1], s - t)
    return out


def kernel(
    pop, solid, out, f0, f1, flag, sp, u, gq, gvp, gv, gwp, gw, post,
    ys, yr, xs, xr, xys, xyr, zs, zr, xzs, xzr, sem_in, send, recv,
):
    ix, iy, iz = lax.axis_index("gx"), lax.axis_index("gy"), lax.axis_index("gz")
    nx, ny, nz = lax.axis_size("gx"), lax.axis_size("gy"), lax.axis_size("gz")
    xd = ({"gx": lax.rem(ix + 1, nx)}, {"gx": lax.rem(ix + nx - 1, nx)})
    yd = ({"gy": lax.rem(iy + 1, ny)}, {"gy": lax.rem(iy + ny - 1, ny)})
    zd = ({"gz": lax.rem(iz + 1, nz)}, {"gz": lax.rem(iz + nz - 1, nz)})

    barrier = pltpu.get_barrier_semaphore()
    for target in (*zd, *xd, *yd):
        pl.semaphore_signal(barrier, inc=1, device_id=target, device_id_type=MESH)
    loads = [
        pltpu.make_async_copy(solid, flag, sem_in.at[0]),
        pltpu.make_async_copy(pop.at[0], f0, sem_in.at[1]),
        pltpu.make_async_copy(pop.at[1], f1.at[:, 1:5, 0:16, :], sem_in.at[2]),
    ]
    for copy in loads:
        copy.start()

    slots = iter(range(12))

    def remote(src, dst, target):
        n = next(slots)
        return pltpu.make_async_remote_copy(
            src_ref=src, dst_ref=dst, send_sem=send.at[n], recv_sem=recv.at[n], device_id=target, device_id_type=MESH
        )

    for copy in loads:
        copy.wait()

    for x in range(NX_L):
        fluid = flag[x] == 0
        rho, momentum = [], []
        for k in range(2):
            f = (lambda i: f0[i, x]) if k == 0 else (lambda i: f1[i, x + 1, 0:16, :])
            total = f(0)
            mom = [None, None, None]
            for i, j in PAIRS:
                a, b = f(i), f(j)
                total = total + (a + b)
                d = a - b
                for axis in range(3):
                    c = VELOCITIES[i][axis]
                    if c:
                        mom[axis] = d * float(c) if mom[axis] is None else (mom[axis] + d if c > 0 else mom[axis] - d)
            rho.append(total)
            momentum.append(mom)
            sp[k, x + 2, 0:16, :] = jnp.where(fluid, total, -wall_values[k])
        inv = 1.0 / (rho[0] * (1.0 / relax_times[0]) + rho[1] * (1.0 / relax_times[1]))
        for axis in range(3):
            u[axis, x + 1, 0:16, :] = (
                momentum[0][axis] * (1.0 / relax_times[0]) + momentum[1][axis] * (1.0 / relax_times[1])
            ) * inv

    for s in range(2):
        edge, two = ((15, 14), (0, 0))[s]
        for k in range(2):
            for x in range(NX_L):
                r = (k * 4 + x) * 2
                ys[s, r : r + 2, :] = sp[k, x + 2, two : two + 2, :]
        for axis in range(3):
            for x in range(NX_L):
                r = 16 + axis * 4 + x
                ys[s, r : r + 1, :] = u[axis, x + 1, edge : edge + 1, :]
        for j, i in enumerate(Y_DIRS[s]):
            for x in range(NX_L):
                r = 28 + j * 4 + x
                ys[s, r : r + 1, :] = f1[i, x + 1, edge : edge + 1, :]
        for k in range(2):
            for layer in range(2):
                xs[s, k * 2 + layer] = sp[k, 2 + (2 + layer if s == 0 else layer), 0:16, :]
        last = 4 if s == 0 else 1
        for axis in range(3):
            xs[s, 4 + axis] = u[axis, last, 0:16, :]
        for j, i in enumerate(X_DIRS[s]):
            xs[s, 7 + j] = f1[i, last, 0:16, :]

    pl.semaphore_wait(barrier, 6)
    y_copies = [remote(ys.at[s], yr.at[s], yd[s]) for s in range(2)]
    x_copies = [remote(xs.at[s], xr.at[s], xd[s]) for s in range(2)]
    for copy in (*y_copies, *x_copies):
        copy.start()

    lane = lax.broadcasted_iota(jnp.int32, (ROWS, NZ_L), 1)
    tail = lax.broadcasted_iota(jnp.int32, (8, NZ_L), 0)

    for copy in y_copies:
        copy.wait_recv()
    for s in range(2):
        edge, two = ((23, 22), (16, 16))[s]
        for k in range(2):
            for x in range(NX_L):
                r = (k * 4 + x) * 2
                sp[k, x + 2, two : two + 2, :] = yr[s, r : r + 2, :]
        for axis in range(3):
            for x in range(NX_L):
                r = 16 + axis * 4 + x
                u[axis, x + 1, edge : edge + 1, :] = yr[s, r : r + 1, :]
        for j, i in enumerate(Y_DIRS[s]):
            for x in range(NX_L):
                r = 28 + j * 4 + x
                f1[i, x + 1, edge : edge + 1, :] = yr[s, r : r + 1, :]

    for s in range(2):
        near, far = ((127, 126), (0, 1))[s]
        dirs = (Z_LOW, Z_HIGH)[s]
        tile = jnp.zeros((ROWS, NZ_L), jnp.float32)
        for v in range(12):
            for x in range(NX_L):
                if v < 4:
                    value, column = sp[v % 2, x + 2], near if v < 2 else far
                elif v < 7:
                    value, column = u[v - 4, x + 1], near
                else:
                    value, column = f1[dirs[v - 7], x + 1], near
                spot = v * 8 + x + 2
                tile = jnp.where(lane == spot, roll(value, spot - column, 1), tile)
        zs[s] = tile
    z_copies = [remote(zs.at[s], zr.at[s], zd[s]) for s in range(2)]
    for copy in z_copies:
        copy.start()
    for s in range(2):
        last = 4 if s == 0 else 1
        for k in range(2):
            for layer in range(2):
                xys[s, k * 2 + layer] = sp[k, 2 + (2 + layer if s == 0 else layer), 16:24, :]
        for axis in range(3):
            xys[s, 4 + axis] = u[axis, last, 16:24, :]
        up, down = ((7, 9), (10, 8))[s]
        xys[s, 7] = jnp.where(tail < 4, f1[down, last, 16:24, :], f1[up, last, 16:24, :])
    xy_copies = [remote(xys.at[s], xyr.at[s], xd[s]) for s in range(2)]
    own_copies = [remote(zs, xzs.at[s], xd[s]) for s in range(2)]
    for copy in (*xy_copies, *own_copies):
        copy.start()

    for copy in z_copies:
        copy.wait_recv()
    xz_copies = [remote(zr, xzr.at[s], xd[s]) for s in range(2)]
    for copy in xz_copies:
        copy.start()

    for copy in (*x_copies, *xy_copies):
        copy.wait_recv()
    for s in range(2):
        last = 0 if s == 0 else 5
        for k in range(2):
            for layer in range(2):
                plane = layer if s == 0 else 6 + layer
                sp[k, plane, 0:16, :] = xr[s, k * 2 + layer]
                sp[k, plane, 16:24, :] = xyr[s, k * 2 + layer]
        for axis in range(3):
            u[axis, last, 0:16, :] = xr[s, 4 + axis]
            u[axis, last, 16:24, :] = xyr[s, 4 + axis]
        for j, i in enumerate(X_DIRS[s]):
            f1[i, last, 0:16, :] = xr[s, 7 + j]
            if VELOCITIES[i][1]:
                f1[i, last, 16:24, :] = xyr[s, 7]

    for copy in (*own_copies, *xz_copies):
        copy.wait_recv()

    part = lane % 8

    def merged(own, low, high):
        return jnp.where(part < 2, roll(low, -4, 1), jnp.where(part > 5, roll(high, 4, 1), own))

    low = merged(zr[0], xzr[0, 0], xzr[1, 0])
    high = merged(zr[1], xzr[0, 1], xzr[1, 1])
    own_low = merged(zs[1], xzs[0, 1], xzs[1, 1])
    own_high = merged(zs[0], xzs[0, 0], xzs[1, 0])

    for k in range(2):
        for p in range(8):
            a = jnp.abs(sp[k, p])
            above = jnp.where(lane == 127, roll(jnp.abs(high), 127 - (k * 8 + p), 1), roll(a, -1, 1))
            below = jnp.where(lane == 0, roll(jnp.abs(low), -(k * 8 + p), 1), roll(a, 1, 1))
            pz, w = above + below, above - below
            a_up, a_down = roll(a, -1, 0), roll(a, 1, 0)
            gq[k, p] = FACE * a + DIAG * (a_up + a_down + pz)
            v = a_up - a_down
            gv[k, p] = DIAG * v
            gw[k, p] = DIAG * w
            if 1 <= p <= 6:
                gvp[k, p] = FACE * v + DIAG * (roll(pz, -1, 0) - roll(pz, 1, 0))
                gwp[k, p] = FACE * w + DIAG * (roll(w, -1, 0) + roll(w, 1, 0))

    for p in range(1, 7):
        grad = [
            (
                gq[k, p + 1] - gq[k, p - 1],
                gvp[k, p] + gv[k, p + 1] + gv[k, p - 1],
                gwp[k, p] + gw[k, p + 1] + gw[k, p - 1],
            )
            for k in range(2)
        ]
        dirs = X_DIRS[0] if p == 1 else X_DIRS[1] if p == 6 else list(range(19))
        for k in range(2):
            value = sp[k, p]
            vel = [u[axis, p - 1] - (coupling * relax_times[k]) * grad[1 - k][axis] for axis in range(3)]
            for i, item in posts(k, value > 0.0, value, vel, dirs, lambda i: f1[i, p - 1]).items():
                post[k, i, p - 1] = item

    def both(a, va, b, vb):
        return jnp.where(lane < 8, roll(a, -8 * va, 1), roll(b, 8 - 8 * vb, 1))

    value = [both(low, k, high, k) for k in range(2)]
    grad = []
    for k in range(2):
        a = jnp.abs(value[k])
        below = jnp.abs(both(low, 2 + k, own_high, k))
        above = jnp.abs(both(own_low, k, high, 2 + k))
        pz, w = above + below, above - below
        a_up, a_down = roll(a, -1, 0), roll(a, 1, 0)
        q = FACE * a + DIAG * (a_up + a_down + pz)
        v = a_up - a_down
        grad.append(
            (
                roll(q, -1, 1) - roll(q, 1, 1),
                FACE * v + DIAG * (roll(pz, -1, 0) - roll(pz, 1, 0) + roll(v, -1, 1) + roll(v, 1, 1)),
                FACE * w + DIAG * (roll(w, -1, 0) + roll(w, 1, 0) + roll(w, -1, 1) + roll(w, 1, 1)),
            )
        )
    sign = jnp.where(lane < 8, 1.0, -1.0)
    common = [both(low, 4 + axis, high, 4 + axis) for axis in range(3)]
    beyond = [
        posts(
            k,
            value[k] > 0.0,
            jnp.abs(value[k]),
            [sign * (common[axis] - (coupling * relax_times[k]) * grad[1 - k][axis]) for axis in range(3)],
            Z_LOW,
            lambda i: both(low, 7 + Z_LOW.index(i), high, 7 + Z_LOW.index(i)),
        )
        for k in range(2)
    ]

    lane16 = lax.broadcasted_iota(jnp.int32, (NY_L, NZ_L), 1)
    for k in range(2):
        for i in range(19):
            cx, cy, cz = VELOCITIES[i]
            if cz:
                side = beyond[k][i if cz > 0 else OPPOSITE[i]]
                side = (roll(side, cy, 0) if cy else side)[0:16]
            for x in range(NX_L):
                fluid = flag[x] == 0
                old = f0[i, x] if k == 0 else f1[i, x + 1, 0:16, :]
                if i == 0:
                    moved = post[k, 0, x + 1, 0:16, :]
                else:
                    moved = post[k, i, x + 1 - cx]
                    moved = (roll(moved, cy, 0) if cy else moved)[0:16]
                    if cz > 0:
                        moved = jnp.where(lane16 == 0, roll(side, -(x - cx + 2), 1), roll(moved, 1, 1))
                    elif cz < 0:
                        moved = jnp.where(lane16 == 127, roll(side, 127 - (x - cx + 10), 1), roll(moved, -1, 1))
                    moved = jnp.where(moved < LIMIT, moved, post[k, OPPOSITE[i], x + 1, 0:16, :])
                out[k, i, x] = jnp.where(fluid, moved, old)

    for copy in (*y_copies, *x_copies, *z_copies, *xy_copies, *own_copies, *xz_copies):
        copy.wait_send()


def body(populations, solid):
    f32 = jnp.float32
    plane = (ROWS, NZ_L)
    scratch = [
        pltpu.VMEM((19, 4, 16, 128), f32),
        pltpu.VMEM((19, 6, *plane), f32),
        pltpu.VMEM((4, 16, 128), jnp.int32),
        pltpu.VMEM((2, 8, *plane), f32),
        pltpu.VMEM((3, 6, *plane), f32),
        *[pltpu.VMEM((2, 8, *plane), f32)] * 5,
        pltpu.VMEM((2, 19, 6, *plane), f32),
        *[pltpu.VMEM((2, 48, 128), f32)] * 2,
        *[pltpu.VMEM((2, 12, 16, 128), f32)] * 2,
        *[pltpu.VMEM((2, 8, 8, 128), f32)] * 2,
        *[pltpu.VMEM((2, *plane), f32)] * 2,
        *[pltpu.VMEM((2, 2, *plane), f32)] * 2,
        pltpu.SemaphoreType.DMA((3,)),
        pltpu.SemaphoreType.DMA((12,)),
        pltpu.SemaphoreType.DMA((12,)),
    ]
    return pl.pallas_call(
        kernel,
        out_shape=jax.ShapeDtypeStruct(populations.shape, f32),
        in_specs=[pl.BlockSpec(memory_space=pl.ANY)] * 2,
        out_specs=pl.BlockSpec(memory_space=pltpu.VMEM),
        scratch_shapes=scratch,
        compiler_params=pltpu.CompilerParams(
            collective_id=0, has_side_effects=True, vmem_limit_bytes=40 * 1024 * 1024
        ),
    )(populations, solid)


def solution(mesh):
    in_specs = (P(None, None, "gx", "gy", "gz"), P("gx", "gy", "gz"))
    out_specs = P(None, None, "gx", "gy", "gz")
    return jax.shard_map(body, mesh=mesh, in_specs=in_specs, out_specs=out_specs, check_vma=False)
```

time: 124 us -> 30.7 us (0.25)
  starting transfers between devices: 51.3 us -> 0 us
  waiting for transfers between devices: 34.1 us -> 0 us
  Pallas kernels: 0 us -> 27.4 us
  local copies, waits for them, and re-layouts: 21.4 us -> 3.09 us
  other arithmetic: 12.5 us -> 0 us
  matrix products: 3.77 us -> 0 us
    ppermute x12 -> x0, starting transfers between devices: 51.3 us -> none  [the longest x6 27.1 us: extended(): lax.ppermute(lax.slice_in_dim(block, 0, width, axis=dim), axis, backward)]
    ppermute x12 -> x0, waiting for transfers between devices: 34.1 us -> none  [the longest x6 25.1 us: extended(): lax.ppermute(lax.slice_in_dim(block, block.shape[dim] - width, None, axis...]
    pallas_call x0 -> x1, Pallas kernels: none -> 27.4 us  [body(): pl.pallas_call(kernel, out_shape=jax.ShapeDtypeStruct(populations.shape,...]
    slice x9 -> x0, local copies, waits for them, and re-layouts: 10.4 us -> none  [the longest x5 6.56 us: extended(): lax.slice_in_dim(block, block.shape[dim] - width, None, axis=dim)]
    ppermute x2 -> x0, local copies, waits for them, and re-layouts: 7.36 us -> none  [the longest x1 4.15 us: extended(): lax.ppermute(lax.slice_in_dim(block, 0, width, axis=dim), axis, backward)]
    concatenate x3 -> x0, other arithmetic: 6.5 us -> none  [extended(): block = jnp.concatenate([low, block, high], axis=dim)]
    dot_general x3 -> x0, matrix products: 3.77 us -> none  [the longest x2 2.16 us: collide(): jnp.einsum('ia,axyz->ixyz', vel, velocity, precision=lax.Precision.HIGHEST)]
    reduce_sum x2 -> x0, other arithmetic: 1.67 us -> none  [the longest x1 1.37 us: body(): rho = jnp.sum(populations, axis=1)]
  transfers between devices with their start and end apart: 12 -> 0, of which waited for: 9 -> 0; matrix products, arithmetic and copies ran while one was open for 5% -> 0% of each run, Pallas kernels for 0% -> 0%
where the time goes in v1:
time: 30.7 us; the launch traced here: 30.5 us
  Pallas kernels  27.4 us (89%)
  local copies, waits for them, and re-layouts  3.09 us (10%)
    pallas_call x1, Pallas kernels, body(): pl.pallas_call(kernel, out_shape=jax.ShapeDtypeStruct(populations.shape,...  27.4 us
    unnamed x5, local copies, waits for them, and re-layouts  3.09 us

profile of v1, /device:TPU:1, one launch (start us, length us, event | category | flops | bytes accessed | tf_op | source)
XLA Modules:
  0.0 30.5 jit_solution(3516741850573598661)
XLA Ops:
  0.0 0.0 copy-start
  0.0 1.3 %copy-done = f32[2,19,4,16,128]{4,3,2,1,0:T(8,128)S(1)} copy-done((f32[2,19,4,16,128]{4,3,2,1,0:T(8,128)S(1)}, f32[2,19,4,16,128]{4,3,2,1,0:T(8,128)}, u32[]{:S(2)}) %copy-start) | copy-done | bytes 1245208
  1.3 0.0 copy-start.1
  1.3 0.8 %copy-done.1 = s32[4,16,128]{2,1,0:T(8,128)S(1)} copy-done((s32[4,16,128]{2,1,0:T(8,128)S(1)}, s32[4,16,128]{2,1,0:T(8,128)}, u32[]{:S(2)}) %copy-start.1) | copy-done | bytes 32792
  2.1 27.4 %shard_map.28 = f32[2,19,4,16,128]{4,3,2,1,0:T(8,128)S(1)} custom-call(f32[2,19,4,16,128]{4,3,2,1,0:T(8,128)S(1)} %copy-done, s32[4,16,128]{2,1,0:T(8,128)S(1)} %copy-done.1), custom_call_target="tpu_custom_call" | custom-call | tf_op jit(solution)/shard_map/pallas_call | solution.py:375
  29.5 1.0 %copy.4 = f32[2,19,4,16,128]{4,3,2,1,0:T(8,128)} copy(f32[2,19,4,16,128]{4,3,2,1,0:T(8,128)S(1)} %shard_map.28) | data formatting | bytes 2490368
Async XLA Ops:
  0.0 1.3 %copy-start = (f32[2,19,4,16,128]{4,3,2,1,0:T(8,128)S(1)}, f32[2,19,4,16,128]{4,3,2,1,0:T(8,128)}, u32[]{:S(2)}) copy-start(f32[2,19,4,16,128]{4,3,2,1,0:T(8,128)} %pop.1) | copy-start | bytes 3735556
  1.3 0.8 %copy-start.1 = (s32[4,16,128]{2,1,0:T(8,128)S(1)}, s32[4,16,128]{2,1,0:T(8,128)}, u32[]{:S(2)}) copy-start(s32[4,16,128]{2,1,0:T(8,128)} %solid.1) | copy-start | bytes 98308

commit v2 on v1

--- a/solution.py
+++ b/solution.py
@@ -88,33 +88,76 @@
     return out
 
 
+def index_of(c):
+    return 0 if c > 0 else 1
+
+
+def ahead(ix, iz, nx, nz, dx, dz):
+    if dz:
+        rank = (lambda g: jnp.where(g < 2, g, 5 - g)) if nz == 4 else (lambda g: g)
+        return rank(iz) > rank(lax.rem(iz + dz + nz, nz))
+    if dx:
+        return lax.rem(ix, 4) > lax.rem(lax.rem(ix + dx + nx, nx), 4)
+    return None
+
+
 def kernel(
-    pop, solid, out, f0, f1, flag, sp, u, gq, gvp, gv, gwp, gw, post,
-    ys, yr, xs, xr, xys, xyr, zs, zr, xzs, xzr, sem_in, send, recv,
+    pop, flag, out, f0, f1, sp, u, gq, gvp, gv, gwp, gw, post,
+    ys, yr, xs, xr, xys, xyr, tile, zs, zr, xzr, ps, yzr, xyzr, rest, sem_in, send, recv,
 ):
     ix, iy, iz = lax.axis_index("gx"), lax.axis_index("gy"), lax.axis_index("gz")
     nx, ny, nz = lax.axis_size("gx"), lax.axis_size("gy"), lax.axis_size("gz")
-    xd = ({"gx": lax.rem(ix + 1, nx)}, {"gx": lax.rem(ix + nx - 1, nx)})
-    yd = ({"gy": lax.rem(iy + 1, ny)}, {"gy": lax.rem(iy + ny - 1, ny)})
-    zd = ({"gz": lax.rem(iz + 1, nz)}, {"gz": lax.rem(iz + nz - 1, nz)})
-
-    barrier = pltpu.get_barrier_semaphore()
-    for target in (*zd, *xd, *yd):
-        pl.semaphore_signal(barrier, inc=1, device_id=target, device_id_type=MESH)
+    around = (0, 1, -1)
+    groups = [(dx, dz) for dz in (1, -1) for dx in around] + [(1, 0), (-1, 0)]
+    sends_first = {g: ahead(ix, iz, nx, nz, *g) for g in groups}
+
+    def target(dx, dy, dz):
+        place = {}
+        if dx:
+            place["gx"] = lax.rem(ix + dx + nx, nx)
+        if dy:
+            place["gy"] = lax.rem(iy + dy + ny, ny)
+        if dz:
+            place["gz"] = lax.rem(iz + dz + nz, nz)
+        return place
+
     loads = [
-        pltpu.make_async_copy(solid, flag, sem_in.at[0]),
-        pltpu.make_async_copy(pop.at[0], f0, sem_in.at[1]),
-        pltpu.make_async_copy(pop.at[1], f1.at[:, 1:5, 0:16, :], sem_in.at[2]),
+        pltpu.make_async_copy(pop.at[0], f0, sem_in.at[0]),
+        pltpu.make_async_copy(pop.at[1], f1.at[:, 1:5, 0:16, :], sem_in.at[1]),
     ]
     for copy in loads:
         copy.start()
-
-    slots = iter(range(12))
-
-    def remote(src, dst, target):
-        n = next(slots)
-        return pltpu.make_async_remote_copy(
-            src_ref=src, dst_ref=dst, send_sem=send.at[n], recv_sem=recv.at[n], device_id=target, device_id_type=MESH
+    barrier = pltpu.get_barrier_semaphore()
+    count = 2
+    for dx, dz in groups:
+        first = sends_first[dx, dz]
+        count = count + 3 * first.astype(jnp.int32)
+
+        @pl.when(jnp.logical_not(first))
+        def _(dx=dx, dz=dz):
+            for dy in around:
+                pl.semaphore_signal(barrier, inc=1, device_id=target(dx, dy, dz), device_id_type=MESH)
+
+    for dy in (1, -1):
+        pl.semaphore_signal(barrier, inc=1, device_id=target(0, dy, 0), device_id_type=MESH)
+
+    ways = [(dx, dy, dz) for dz in around for dx in around for dy in around if dx or dy or dz]
+    copies = {}
+    for n, (dx, dy, dz) in enumerate(ways):
+        x, y, z = index_of(dx), index_of(dy), index_of(dz)
+        if dz:
+            src = ps.at[z, y] if dy else zs.at[z]
+            if dx:
+                dst = xyzr.at[x, y, z] if dy else xzr.at[x, z]
+            else:
+                dst = yzr.at[y, z] if dy else zr.at[z]
+        elif dx:
+            src, dst = (xys.at[x, y], xyr.at[x, y]) if dy else (xs.at[x], xr.at[x])
+        else:
+            src, dst = ys.at[y], yr.at[y]
+        copies[dx, dy, dz] = pltpu.make_async_remote_copy(
+            src_ref=src, dst_ref=dst, send_sem=send.at[n], recv_sem=recv.at[n],
+            device_id=target(dx, dy, dz), device_id_type=MESH,
         )
 
     for copy in loads:
@@ -144,6 +187,52 @@
                 momentum[0][axis] * (1.0 / relax_times[0]) + momentum[1][axis] * (1.0 / relax_times[1])
             ) * inv
 
+    lane = lax.broadcasted_iota(jnp.int32, (ROWS, NZ_L), 1)
+    lane16 = lax.broadcasted_iota(jnp.int32, (NY_L, NZ_L), 1)
+    part = lax.broadcasted_iota(jnp.int32, (8, NZ_L), 1) % 8
+
+    for s in range(2):
+        near, far = ((127, 126), (0, 1))[s]
+        dirs = (Z_LOW, Z_HIGH)[s]
+        packed = jnp.zeros((NY_L, NZ_L), jnp.float32)
+        for v in range(12):
+            for x in range(NX_L):
+                if v < 4:
+                    value, column = sp[v % 2, x + 2, 0:16, :], near if v < 2 else far
+                elif v < 7:
+                    value, column = u[v - 4, x + 1, 0:16, :], near
+                else:
+                    value, column = f1[dirs[v - 7], x + 1, 0:16, :], near
+                spot = v * 8 + x + 2
+                packed = jnp.where(lane16 == spot, roll(value, spot - column, 1), packed)
+        tile[s] = packed
+        zs[s] = jnp.where((part >= 2) & (part <= 5), packed[0:8], roll(packed[8:16], 4, 1))
+        ps[s, 0] = packed[14:16]
+        ps[s, 1] = packed[0:2]
+
+    def start_first(group):
+        @pl.when(sends_first[group])
+        def _():
+            for dy in around:
+                copies[group[0], dy, group[1]].start()
+
+    def answer(group):
+        @pl.when(jnp.logical_not(sends_first[group]))
+        def _():
+            for dy in around:
+                copies[-group[0], -dy, -group[1]].wait_recv()
+                copies[group[0], dy, group[1]].start()
+
+    def collect(group):
+        @pl.when(sends_first[group])
+        def _():
+            for dy in around:
+                copies[-group[0], -dy, -group[1]].wait_recv()
+
+    pl.semaphore_wait(barrier, count)
+    for group in groups[:6]:
+        start_first(group)
+
     for s in range(2):
         edge, two = ((15, 14), (0, 0))[s]
         for k in range(2):
@@ -158,26 +247,40 @@
             for x in range(NX_L):
                 r = 28 + j * 4 + x
                 ys[s, r : r + 1, :] = f1[i, x + 1, edge : edge + 1, :]
-        for k in range(2):
-            for layer in range(2):
-                xs[s, k * 2 + layer] = sp[k, 2 + (2 + layer if s == 0 else layer), 0:16, :]
+        for side in range(2):
+            ys[s, 48 + 2 * side : 50 + 2 * side, :] = tile[side, two : two + 2, :]
+    for dy in (1, -1):
+        copies[0, dy, 0].start()
+    for s in range(2):
         last = 4 if s == 0 else 1
+        planes = [(k, 2 + (2 + layer if s == 0 else layer)) for k in range(2) for layer in range(2)]
+        for n, (k, plane) in enumerate(planes):
+            xs[s, n] = sp[k, plane, 0:16, :]
         for axis in range(3):
             xs[s, 4 + axis] = u[axis, last, 0:16, :]
         for j, i in enumerate(X_DIRS[s]):
             xs[s, 7 + j] = f1[i, last, 0:16, :]
-
-    pl.semaphore_wait(barrier, 6)
-    y_copies = [remote(ys.at[s], yr.at[s], yd[s]) for s in range(2)]
-    x_copies = [remote(xs.at[s], xr.at[s], xd[s]) for s in range(2)]
-    for copy in (*y_copies, *x_copies):
-        copy.start()
-
-    lane = lax.broadcasted_iota(jnp.int32, (ROWS, NZ_L), 1)
-    tail = lax.broadcasted_iota(jnp.int32, (8, NZ_L), 0)
-
-    for copy in y_copies:
-        copy.wait_recv()
+        for side in range(2):
+            xs[s, 12 + side] = tile[side]
+        for t in range(2):
+            edge, two = ((15, 14), (0, 0))[t]
+            for n, (k, plane) in enumerate(planes):
+                xys[s, t, 2 * n : 2 * n + 2, :] = sp[k, plane, two : two + 2, :]
+            for axis in range(3):
+                xys[s, t, 8 + axis : 9 + axis, :] = u[axis, last, edge : edge + 1, :]
+            i = VELOCITIES.index((1 - 2 * s, 1 - 2 * t, 0))
+            xys[s, t, 11:12, :] = f1[i, last, edge : edge + 1, :]
+            for side in range(2):
+                xys[s, t, 12 + 2 * side : 14 + 2 * side, :] = tile[side, two : two + 2, :]
+    for group in groups[6:]:
+        start_first(group)
+    for group in (*groups[6:], *groups[:6]):
+        answer(group)
+    for dy in (1, -1):
+        copies[0, dy, 0].wait_recv()
+    for group in (*groups[6:], *groups[:6]):
+        collect(group)
+
     for s in range(2):
         edge, two = ((23, 22), (16, 16))[s]
         for k in range(2):
@@ -192,74 +295,60 @@
             for x in range(NX_L):
                 r = 28 + j * 4 + x
                 f1[i, x + 1, edge : edge + 1, :] = yr[s, r : r + 1, :]
-
-    for s in range(2):
-        near, far = ((127, 126), (0, 1))[s]
-        dirs = (Z_LOW, Z_HIGH)[s]
-        tile = jnp.zeros((ROWS, NZ_L), jnp.float32)
-        for v in range(12):
-            for x in range(NX_L):
-                if v < 4:
-                    value, column = sp[v % 2, x + 2], near if v < 2 else far
-                elif v < 7:
-                    value, column = u[v - 4, x + 1], near
-                else:
-                    value, column = f1[dirs[v - 7], x + 1], near
-                spot = v * 8 + x + 2
-                tile = jnp.where(lane == spot, roll(value, spot - column, 1), tile)
-        zs[s] = tile
-    z_copies = [remote(zs.at[s], zr.at[s], zd[s]) for s in range(2)]
-    for copy in z_copies:
-        copy.start()
-    for s in range(2):
-        last = 4 if s == 0 else 1
-        for k in range(2):
-            for layer in range(2):
-                xys[s, k * 2 + layer] = sp[k, 2 + (2 + layer if s == 0 else layer), 16:24, :]
-        for axis in range(3):
-            xys[s, 4 + axis] = u[axis, last, 16:24, :]
-        up, down = ((7, 9), (10, 8))[s]
-        xys[s, 7] = jnp.where(tail < 4, f1[down, last, 16:24, :], f1[up, last, 16:24, :])
-    xy_copies = [remote(xys.at[s], xyr.at[s], xd[s]) for s in range(2)]
-    own_copies = [remote(zs, xzs.at[s], xd[s]) for s in range(2)]
-    for copy in (*xy_copies, *own_copies):
-        copy.start()
-
-    for copy in z_copies:
-        copy.wait_recv()
-    xz_copies = [remote(zr, xzr.at[s], xd[s]) for s in range(2)]
-    for copy in xz_copies:
-        copy.start()
-
-    for copy in (*x_copies, *xy_copies):
-        copy.wait_recv()
     for s in range(2):
         last = 0 if s == 0 else 5
-        for k in range(2):
-            for layer in range(2):
-                plane = layer if s == 0 else 6 + layer
-                sp[k, plane, 0:16, :] = xr[s, k * 2 + layer]
-                sp[k, plane, 16:24, :] = xyr[s, k * 2 + layer]
+        planes = [(k, layer if s == 0 else 6 + layer) for k in range(2) for layer in range(2)]
+        for n, (k, plane) in enumerate(planes):
+            sp[k, plane, 0:16, :] = xr[s, n]
         for axis in range(3):
             u[axis, last, 0:16, :] = xr[s, 4 + axis]
-            u[axis, last, 16:24, :] = xyr[s, 4 + axis]
         for j, i in enumerate(X_DIRS[s]):
             f1[i, last, 0:16, :] = xr[s, 7 + j]
-            if VELOCITIES[i][1]:
-                f1[i, last, 16:24, :] = xyr[s, 7]
-
-    for copy in (*own_copies, *xz_copies):
-        copy.wait_recv()
-
-    part = lane % 8
-
-    def merged(own, low, high):
-        return jnp.where(part < 2, roll(low, -4, 1), jnp.where(part > 5, roll(high, 4, 1), own))
-
-    low = merged(zr[0], xzr[0, 0], xzr[1, 0])
-    high = merged(zr[1], xzr[0, 1], xzr[1, 1])
-    own_low = merged(zs[1], xzs[0, 1], xzs[1, 1])
-    own_high = merged(zs[0], xzs[0, 0], xzs[1, 0])
+        for t in range(2):
+            edge, two = ((23, 22), (16, 16))[t]
+            for n, (k, plane) in enumerate(planes):
+                sp[k, plane, two : two + 2, :] = xyr[s, t, 2 * n : 2 * n + 2, :]
+            for axis in range(3):
+                u[axis, last, edge : edge + 1, :] = xyr[s, t, 8 + axis : 9 + axis, :]
+            i = VELOCITIES.index((1 - 2 * s, 1 - 2 * t, 0))
+            f1[i, last, edge : edge + 1, :] = xyr[s, t, 11:12, :]
+
+    def merged(own, below, above):
+        return jnp.where(part < 2, below, jnp.where(part > 5, above, own))
+
+    def row_tile(n, after, before):
+        rest[n, 6:8, :] = before
+        rest[n, 0:2, :] = after
+        return rest[n]
+
+    def beyond_z(side):
+        own, a, b = zr[side], xzr[0, side], xzr[1, side]
+        n = side * 3
+        third = merged(
+            row_tile(n, yzr[1, side], yzr[0, side]),
+            roll(row_tile(n + 1, xyzr[0, 1, side], xyzr[0, 0, side]), -4, 1),
+            roll(row_tile(n + 2, xyzr[1, 1, side], xyzr[1, 0, side]), 4, 1),
+        )
+        return jnp.concatenate(
+            [merged(own, roll(a, -4, 1), roll(b, 4, 1)), merged(roll(own, -4, 1), roll(a, -8, 1), b), third], axis=0
+        )
+
+    def own_z(side):
+        n = 6 + side * 3
+        r, q = slice(48 + 2 * side, 50 + 2 * side), slice(12 + 2 * side, 14 + 2 * side)
+        third = merged(
+            row_tile(n, yr[1, r, :], yr[0, r, :]),
+            roll(row_tile(n + 1, xyr[0, 1, q, :], xyr[0, 0, q, :]), -4, 1),
+            roll(row_tile(n + 2, xyr[1, 1, q, :], xyr[1, 0, q, :]), 4, 1),
+        )
+        rows = [
+            merged(tile[side, h, :], roll(xr[0, 12 + side, h, :], -4, 1), roll(xr[1, 12 + side, h, :], 4, 1))
+            for h in (slice(0, 8), slice(8, 16))
+        ]
+        return jnp.concatenate([*rows, third], axis=0)
+
+    low, high = beyond_z(0), beyond_z(1)
+    own_high, own_low = own_z(0), own_z(1)
 
     for k in range(2):
         for p in range(8):
@@ -326,7 +415,6 @@
         for k in range(2)
     ]
 
-    lane16 = lax.broadcasted_iota(jnp.int32, (NY_L, NZ_L), 1)
     for k in range(2):
         for i in range(19):
             cx, cy, cz = VELOCITIES[i]
@@ -348,7 +436,7 @@
                     moved = jnp.where(moved < LIMIT, moved, post[k, OPPOSITE[i], x + 1, 0:16, :])
                 out[k, i, x] = jnp.where(fluid, moved, old)
 
-    for copy in (*y_copies, *x_copies, *z_copies, *xy_copies, *own_copies, *xz_copies):
+    for copy in copies.values():
         copy.wait_send()
 
 
@@ -358,28 +446,31 @@
     scratch = [
         pltpu.VMEM((19, 4, 16, 128), f32),
         pltpu.VMEM((19, 6, *plane), f32),
-        pltpu.VMEM((4, 16, 128), jnp.int32),
         pltpu.VMEM((2, 8, *plane), f32),
         pltpu.VMEM((3, 6, *plane), f32),
         *[pltpu.VMEM((2, 8, *plane), f32)] * 5,
         pltpu.VMEM((2, 19, 6, *plane), f32),
-        *[pltpu.VMEM((2, 48, 128), f32)] * 2,
-        *[pltpu.VMEM((2, 12, 16, 128), f32)] * 2,
-        *[pltpu.VMEM((2, 8, 8, 128), f32)] * 2,
-        *[pltpu.VMEM((2, *plane), f32)] * 2,
-        *[pltpu.VMEM((2, 2, *plane), f32)] * 2,
-        pltpu.SemaphoreType.DMA((3,)),
-        pltpu.SemaphoreType.DMA((12,)),
-        pltpu.SemaphoreType.DMA((12,)),
+        *[pltpu.VMEM((2, 56, 128), f32)] * 2,
+        *[pltpu.VMEM((2, 14, 16, 128), f32)] * 2,
+        *[pltpu.VMEM((2, 2, 16, 128), f32)] * 2,
+        pltpu.VMEM((2, 16, 128), f32),
+        *[pltpu.VMEM((2, 8, 128), f32)] * 2,
+        pltpu.VMEM((2, 2, 8, 128), f32),
+        *[pltpu.VMEM((2, 2, 2, 128), f32)] * 2,
+        pltpu.VMEM((2, 2, 2, 2, 128), f32),
+        pltpu.VMEM((12, 8, 128), f32),
+        pltpu.SemaphoreType.DMA((2,)),
+        pltpu.SemaphoreType.DMA((26,)),
+        pltpu.SemaphoreType.DMA((26,)),
     ]
     return pl.pallas_call(
         kernel,
         out_shape=jax.ShapeDtypeStruct(populations.shape, f32),
-        in_specs=[pl.BlockSpec(memory_space=pl.ANY)] * 2,
+        in_specs=[pl.BlockSpec(memory_space=pl.ANY), pl.BlockSpec(memory_space=pltpu.VMEM)],
         out_specs=pl.BlockSpec(memory_space=pltpu.VMEM),
         scratch_shapes=scratch,
         compiler_params=pltpu.CompilerParams(
-            collective_id=0, has_side_effects=True, vmem_limit_bytes=40 * 1024 * 1024
+            collective_id=0, has_side_effects=True, vmem_limit_bytes=52 * 1024 * 1024
         ),
     )(populations, solid)
 

time: 30.7 us -> 27.7 us (0.902)
  the two profiles are of different devices: /device:TPU:1 before, /device:TPU:256 now
where the time goes in v2:
time: 27.7 us; the launch traced here: 27.5 us
  Pallas kernels  25.7 us (93%)
  local copies, waits for them, and re-layouts  1.79 us (6%)
    pallas_call x1, Pallas kernels, body(): pl.pallas_call(kernel, out_shape=jax.ShapeDtypeStruct(populations.shape,...  25.7 us
    unnamed x3, local copies, waits for them, and re-layouts  1.79 us

profile of v2, /device:TPU:256, one launch (start us, length us, event | category | flops | bytes accessed | tf_op | source)
XLA Modules:
  0.0 27.5 jit_solution(16717397009931836624)
XLA Ops:
  0.0 0.0 copy-start
  0.0 0.8 %copy-done = s32[4,16,128]{2,1,0:T(8,128)S(1)} copy-done((s32[4,16,128]{2,1,0:T(8,128)S(1)}, s32[4,16,128]{2,1,0:T(8,128)}, u32[]{:S(2)}) %copy-start) | copy-done | bytes 32792
  0.8 25.7 %shard_map.28 = f32[2,19,4,16,128]{4,3,2,1,0:T(8,128)S(1)} custom-call(f32[2,19,4,16,128]{4,3,2,1,0:T(8,128)} %pop.1, s32[4,16,128]{2,1,0:T(8,128)S(1)} %copy-done), custom_call_target="tpu_custom_call" | custom-call | tf_op jit(solution)/shard_map/pallas_call | solution.py:466
  26.5 1.0 %copy.4 = f32[2,19,4,16,128]{4,3,2,1,0:T(8,128)} copy(f32[2,19,4,16,128]{4,3,2,1,0:T(8,128)S(1)} %shard_map.28) | data formatting | bytes 2490368
Async XLA Ops:
  0.0 0.8 %copy-start = (s32[4,16,128]{2,1,0:T(8,128)S(1)}, s32[4,16,128]{2,1,0:T(8,128)}, u32[]{:S(2)}) copy-start(s32[4,16,128]{2,1,0:T(8,128)} %flag.1) | copy-start | bytes 98308

commit v3 on v2

--- a/solution.py
+++ b/solution.py
@@ -101,15 +101,23 @@
     return None
 
 
+def both_signal(ix, iz, nx, nz, dx, dz):
+    if dx * dz >= 0:
+        return jnp.bool_(False)
+    return (ix == 0) & (iz == nz - 2) if dz > 0 else (ix == nx - 1) & (iz == nz - 1)
+
+
 def kernel(
-    pop, flag, out, f0, f1, sp, u, gq, gvp, gv, gwp, gw, post,
+    pop, solid, out, flag, f0, f1, sp, u, gq, gvp, gv, gwp, gw, post,
     ys, yr, xs, xr, xys, xyr, tile, zs, zr, xzr, ps, yzr, xyzr, rest, sem_in, send, recv,
 ):
     ix, iy, iz = lax.axis_index("gx"), lax.axis_index("gy"), lax.axis_index("gz")
     nx, ny, nz = lax.axis_size("gx"), lax.axis_size("gy"), lax.axis_size("gz")
     around = (0, 1, -1)
     groups = [(dx, dz) for dz in (1, -1) for dx in around] + [(1, 0), (-1, 0)]
-    sends_first = {g: ahead(ix, iz, nx, nz, *g) for g in groups}
+    leads = {g: ahead(ix, iz, nx, nz, *g) for g in groups}
+    mutual = {g: both_signal(ix, iz, nx, nz, *g) for g in groups}
+    sends_first = {g: leads[g] | mutual[g] for g in groups}
 
     def target(dx, dy, dz):
         place = {}
@@ -122,6 +130,7 @@
         return place
 
     loads = [
+        pltpu.make_async_copy(solid, flag, sem_in.at[2]),
         pltpu.make_async_copy(pop.at[0], f0, sem_in.at[0]),
         pltpu.make_async_copy(pop.at[1], f1.at[:, 1:5, 0:16, :], sem_in.at[1]),
     ]
@@ -133,7 +142,7 @@
         first = sends_first[dx, dz]
         count = count + 3 * first.astype(jnp.int32)
 
-        @pl.when(jnp.logical_not(first))
+        @pl.when(jnp.logical_not(leads[dx, dz]) | mutual[dx, dz])
         def _(dx=dx, dz=dz):
             for dy in around:
                 pl.semaphore_signal(barrier, inc=1, device_id=target(dx, dy, dz), device_id_type=MESH)
@@ -444,6 +453,7 @@
     f32 = jnp.float32
     plane = (ROWS, NZ_L)
     scratch = [
+        pltpu.VMEM((4, 16, 128), jnp.int32),
         pltpu.VMEM((19, 4, 16, 128), f32),
         pltpu.VMEM((19, 6, *plane), f32),
         pltpu.VMEM((2, 8, *plane), f32),
@@ -459,20 +469,20 @@
         *[pltpu.VMEM((2, 2, 2, 128), f32)] * 2,
         pltpu.VMEM((2, 2, 2, 2, 128), f32),
         pltpu.VMEM((12, 8, 128), f32),
-        pltpu.SemaphoreType.DMA((2,)),
+        pltpu.SemaphoreType.DMA((3,)),
         pltpu.SemaphoreType.DMA((26,)),
         pltpu.SemaphoreType.DMA((26,)),
     ]
     return pl.pallas_call(
         kernel,
         out_shape=jax.ShapeDtypeStruct(populations.shape, f32),
-        in_specs=[pl.BlockSpec(memory_space=pl.ANY), pl.BlockSpec(memory_space=pltpu.VMEM)],
+        in_specs=[pl.BlockSpec(memory_space=pltpu.HBM)] * 2,
         out_specs=pl.BlockSpec(memory_space=pltpu.VMEM),
         scratch_shapes=scratch,
         compiler_params=pltpu.CompilerParams(
-            collective_id=0, has_side_effects=True, vmem_limit_bytes=52 * 1024 * 1024
+            collective_id=0, has_side_effects=True, vmem_limit_bytes=40 * 1024 * 1024
         ),
-    )(populations, solid)
+    )(*[pltpu.with_memory_space_constraint(a, pltpu.HBM) for a in (populations, solid)])
 
 
 def solution(mesh):

time: 27.7 us -> 24.8 us (0.90)
  the two profiles are of different devices: /device:TPU:256 before, /device:TPU:1 now
where the time goes in v3:
time: 24.8 us; the launch traced here: 24.7 us
  Pallas kernels  23.6 us (95%)
  local copies, waits for them, and re-layouts  1.04 us (4%)
    pallas_call x1, Pallas kernels, body(): pl.pallas_call(kernel, out_shape=jax.ShapeDtypeStruct(populations.shape,...  23.6 us
    unnamed x1, local copies, waits for them, and re-layouts  1.04 us

profile of v3, /device:TPU:1, one launch (start us, length us, event | category | flops | bytes accessed | tf_op | source)
XLA Modules:
  0.0 24.7 jit_solution(13517359272945819763)
XLA Ops:
  0.0 23.6 %shard_map.28 = f32[2,19,4,16,128]{4,3,2,1,0:T(8,128)S(1)} custom-call(f32[2,19,4,16,128]{4,3,2,1,0:T(8,128)} %pop.1, s32[4,16,128]{2,1,0:T(8,128)} %solid.1), custom_call_target="tpu_custom_call" | custom-call | tf_op jit(solution)/shard_map/pallas_call | solution.py:476
  23.6 1.0 %copy.4 = f32[2,19,4,16,128]{4,3,2,1,0:T(8,128)} copy(f32[2,19,4,16,128]{4,3,2,1,0:T(8,128)S(1)} %shard_map.28) | data formatting | bytes 2490368

commit v4 on v3

--- a/solution.py
+++ b/solution.py
@@ -94,14 +94,14 @@
 
 def ahead(ix, iz, nx, nz, dx, dz):
     if dz:
-        rank = (lambda g: jnp.where(g < 2, g, 5 - g)) if nz == 4 else (lambda g: g)
+        rank = (lambda g: jnp.where(g < 2, g, 5 - g)) if nz == 4 else (lambda g: -g)
         return rank(iz) > rank(lax.rem(iz + dz + nz, nz))
     if dx:
         return lax.rem(ix, 4) > lax.rem(lax.rem(ix + dx + nx, nx), 4)
     return None
 
 
-def both_signal(ix, iz, nx, nz, dx, dz):
+def vouched(ix, iz, nx, nz, dx, dz):
     if dx * dz >= 0:
         return jnp.bool_(False)
     return (ix == 0) & (iz == nz - 2) if dz > 0 else (ix == nx - 1) & (iz == nz - 1)
@@ -109,15 +109,16 @@
 
 def kernel(
     pop, solid, out, flag, f0, f1, sp, u, gq, gvp, gv, gwp, gw, post,
-    ys, yr, xs, xr, xys, xyr, tile, zs, zr, xzr, ps, yzr, xyzr, rest, sem_in, send, recv,
+    ys, yr, xs, xr, xys, xyr, tile, zs, zr, xzr, ps, yzr, xyzr, rest, sem_in, send, recv, go, vouch,
 ):
     ix, iy, iz = lax.axis_index("gx"), lax.axis_index("gy"), lax.axis_index("gz")
     nx, ny, nz = lax.axis_size("gx"), lax.axis_size("gy"), lax.axis_size("gz")
     around = (0, 1, -1)
     groups = [(dx, dz) for dz in (1, -1) for dx in around] + [(1, 0), (-1, 0)]
     leads = {g: ahead(ix, iz, nx, nz, *g) for g in groups}
-    mutual = {g: both_signal(ix, iz, nx, nz, *g) for g in groups}
-    sends_first = {g: leads[g] | mutual[g] for g in groups}
+    told = {g: vouched(ix, iz, nx, nz, *g) for g in groups}
+    sends_first = {g: leads[g] & jnp.logical_not(told[g]) for g in groups}
+    answers = {g: jnp.logical_not(leads[g] | told[g]) for g in groups}
 
     def target(dx, dy, dz):
         place = {}
@@ -129,20 +130,25 @@
             place["gz"] = lax.rem(iz + dz + nz, nz)
         return place
 
+    mask_load = pltpu.make_async_copy(solid, flag, sem_in.at[8])
     loads = [
-        pltpu.make_async_copy(solid, flag, sem_in.at[2]),
-        pltpu.make_async_copy(pop.at[0], f0, sem_in.at[0]),
-        pltpu.make_async_copy(pop.at[1], f1.at[:, 1:5, 0:16, :], sem_in.at[1]),
+        (
+            pltpu.make_async_copy(pop.at[0, :, x], f0.at[:, x], sem_in.at[2 * x]),
+            pltpu.make_async_copy(pop.at[1, :, x], f1.at[:, x + 1, 0:16, :], sem_in.at[2 * x + 1]),
+        )
+        for x in range(NX_L)
     ]
-    for copy in loads:
-        copy.start()
+    mask_load.start()
+    for pair in loads:
+        for copy in pair:
+            copy.start()
     barrier = pltpu.get_barrier_semaphore()
     count = 2
     for dx, dz in groups:
         first = sends_first[dx, dz]
         count = count + 3 * first.astype(jnp.int32)
 
-        @pl.when(jnp.logical_not(leads[dx, dz]) | mutual[dx, dz])
+        @pl.when(answers[dx, dz])
         def _(dx=dx, dz=dz):
             for dy in around:
                 pl.semaphore_signal(barrier, inc=1, device_id=target(dx, dy, dz), device_id_type=MESH)
@@ -169,10 +175,15 @@
             device_id=target(dx, dy, dz), device_id_type=MESH,
         )
 
-    for copy in loads:
-        copy.wait()
-
+    lane = lax.broadcasted_iota(jnp.int32, (ROWS, NZ_L), 1)
+    lane16 = lax.broadcasted_iota(jnp.int32, (NY_L, NZ_L), 1)
+    part = lax.broadcasted_iota(jnp.int32, (8, NZ_L), 1) % 8
+
+    mask_load.wait()
+    packed = [jnp.zeros((NY_L, NZ_L), jnp.float32) for s in range(2)]
     for x in range(NX_L):
+        for copy in loads[x]:
+            copy.wait()
         fluid = flag[x] == 0
         rho, momentum = [], []
         for k in range(2):
@@ -196,16 +207,10 @@
                 momentum[0][axis] * (1.0 / relax_times[0]) + momentum[1][axis] * (1.0 / relax_times[1])
             ) * inv
 
-    lane = lax.broadcasted_iota(jnp.int32, (ROWS, NZ_L), 1)
-    lane16 = lax.broadcasted_iota(jnp.int32, (NY_L, NZ_L), 1)
-    part = lax.broadcasted_iota(jnp.int32, (8, NZ_L), 1) % 8
-
-    for s in range(2):
-        near, far = ((127, 126), (0, 1))[s]
-        dirs = (Z_LOW, Z_HIGH)[s]
-        packed = jnp.zeros((NY_L, NZ_L), jnp.float32)
-        for v in range(12):
-            for x in range(NX_L):
+        for s in range(2):
+            near, far = ((127, 126), (0, 1))[s]
+            dirs = (Z_LOW, Z_HIGH)[s]
+            for v in range(12):
                 if v < 4:
                     value, column = sp[v % 2, x + 2, 0:16, :], near if v < 2 else far
                 elif v < 7:
@@ -213,11 +218,12 @@
                 else:
                     value, column = f1[dirs[v - 7], x + 1, 0:16, :], near
                 spot = v * 8 + x + 2
-                packed = jnp.where(lane16 == spot, roll(value, spot - column, 1), packed)
-        tile[s] = packed
-        zs[s] = jnp.where((part >= 2) & (part <= 5), packed[0:8], roll(packed[8:16], 4, 1))
-        ps[s, 0] = packed[14:16]
-        ps[s, 1] = packed[0:2]
+                packed[s] = jnp.where(lane16 == spot, roll(value, spot - column, 1), packed[s])
+    for s in range(2):
+        tile[s] = packed[s]
+        zs[s] = jnp.where((part >= 2) & (part <= 5), packed[s][0:8], roll(packed[s][8:16], 4, 1))
+        ps[s, 0] = packed[s][14:16]
+        ps[s, 1] = packed[s][0:2]
 
     def start_first(group):
         @pl.when(sends_first[group])
@@ -225,20 +231,32 @@
             for dy in around:
                 copies[group[0], dy, group[1]].start()
 
-    def answer(group):
-        @pl.when(jnp.logical_not(sends_first[group]))
-        def _():
-            for dy in around:
-                copies[-group[0], -dy, -group[1]].wait_recv()
-                copies[group[0], dy, group[1]].start()
-
-    def collect(group):
+    def admit(group):
         @pl.when(sends_first[group])
         def _():
             for dy in around:
-                copies[-group[0], -dy, -group[1]].wait_recv()
+                way = (group[0], dy, group[1])
+                pl.semaphore_signal(go.at[ways.index(way)], inc=1, device_id=target(*way), device_id_type=MESH)
+
+    def answer(group):
+        @pl.when(answers[group])
+        def _():
+            for dy in around:
+                pl.semaphore_wait(go.at[ways.index((-group[0], -dy, -group[1]))], 1)
+                copies[group[0], dy, group[1]].start()
+
+    def collect(group):
+        for dy in around:
+            copies[-group[0], -dy, -group[1]].wait_recv()
 
     pl.semaphore_wait(barrier, count)
+    for group in groups:
+        admit(group)
+
+    @pl.when((ix == nx - 1) & (iz == nz - 2))
+    def _():
+        pl.semaphore_signal(vouch, inc=1, device_id=target(1, 0, 0), device_id_type=MESH)
+        pl.semaphore_signal(vouch, inc=1, device_id=target(0, 0, 1), device_id_type=MESH)
     for group in groups[:6]:
         start_first(group)
 
@@ -283,44 +301,58 @@
                 xys[s, t, 12 + 2 * side : 14 + 2 * side, :] = tile[side, two : two + 2, :]
     for group in groups[6:]:
         start_first(group)
-    for group in (*groups[6:], *groups[:6]):
+    def take_plane():
+        for dy in (1, -1):
+            copies[0, dy, 0].wait_recv()
+        for group in groups[6:]:
+            collect(group)
+        for s in range(2):
+            edge, two = ((23, 22), (16, 16))[s]
+            for k in range(2):
+                for x in range(NX_L):
+                    r = (k * 4 + x) * 2
+                    sp[k, x + 2, two : two + 2, :] = yr[s, r : r + 2, :]
+            for axis in range(3):
+                for x in range(NX_L):
+                    r = 16 + axis * 4 + x
+                    u[axis, x + 1, edge : edge + 1, :] = yr[s, r : r + 1, :]
+            for j, i in enumerate(Y_DIRS[s]):
+                for x in range(NX_L):
+                    r = 28 + j * 4 + x
+                    f1[i, x + 1, edge : edge + 1, :] = yr[s, r : r + 1, :]
+        for s in range(2):
+            last = 0 if s == 0 else 5
+            planes = [(k, layer if s == 0 else 6 + layer) for k in range(2) for layer in range(2)]
+            for n, (k, plane) in enumerate(planes):
+                sp[k, plane, 0:16, :] = xr[s, n]
+            for axis in range(3):
+                u[axis, last, 0:16, :] = xr[s, 4 + axis]
+            for j, i in enumerate(X_DIRS[s]):
+                f1[i, last, 0:16, :] = xr[s, 7 + j]
+            for t in range(2):
+                edge, two = ((23, 22), (16, 16))[t]
+                for n, (k, plane) in enumerate(planes):
+                    sp[k, plane, two : two + 2, :] = xyr[s, t, 2 * n : 2 * n + 2, :]
+                for axis in range(3):
+                    u[axis, last, edge : edge + 1, :] = xyr[s, t, 8 + axis : 9 + axis, :]
+                i = VELOCITIES.index((1 - 2 * s, 1 - 2 * t, 0))
+                f1[i, last, edge : edge + 1, :] = xyr[s, t, 11:12, :]
+
+    for group in groups[6:]:
         answer(group)
-    for dy in (1, -1):
-        copies[0, dy, 0].wait_recv()
-    for group in (*groups[6:], *groups[:6]):
+    for group in groups[:6]:
+        answer(group)
+    for group in ((1, -1), (-1, 1)):
+
+        @pl.when(told[group])
+        def _(group=group):
+            pl.semaphore_wait(vouch, 1)
+            for dy in around:
+                copies[group[0], dy, group[1]].start()
+
+    take_plane()
+    for group in groups[:6]:
         collect(group)
-
-    for s in range(2):
-        edge, two = ((23, 22), (16, 16))[s]
-        for k in range(2):
-            for x in range(NX_L):
-                r = (k * 4 + x) * 2
-                sp[k, x + 2, two : two + 2, :] = yr[s, r : r + 2, :]
-        for axis in range(3):
-            for x in range(NX_L):
-                r = 16 + axis * 4 + x
-                u[axis, x + 1, edge : edge + 1, :] = yr[s, r : r + 1, :]
-        for j, i in enumerate(Y_DIRS[s]):
-            for x in range(NX_L):
-                r = 28 + j * 4 + x
-                f1[i, x + 1, edge : edge + 1, :] = yr[s, r : r + 1, :]
-    for s in range(2):
-        last = 0 if s == 0 else 5
-        planes = [(k, layer if s == 0 else 6 + layer) for k in range(2) for layer in range(2)]
-        for n, (k, plane) in enumerate(planes):
-            sp[k, plane, 0:16, :] = xr[s, n]
-        for axis in range(3):
-            u[axis, last, 0:16, :] = xr[s, 4 + axis]
-        for j, i in enumerate(X_DIRS[s]):
-            f1[i, last, 0:16, :] = xr[s, 7 + j]
-        for t in range(2):
-            edge, two = ((23, 22), (16, 16))[t]
-            for n, (k, plane) in enumerate(planes):
-                sp[k, plane, two : two + 2, :] = xyr[s, t, 2 * n : 2 * n + 2, :]
-            for axis in range(3):
-                u[axis, last, edge : edge + 1, :] = xyr[s, t, 8 + axis : 9 + axis, :]
-            i = VELOCITIES.index((1 - 2 * s, 1 - 2 * t, 0))
-            f1[i, last, edge : edge + 1, :] = xyr[s, t, 11:12, :]
 
     def merged(own, below, above):
         return jnp.where(part < 2, below, jnp.where(part > 5, above, own))
@@ -469,9 +501,11 @@
         *[pltpu.VMEM((2, 2, 2, 128), f32)] * 2,
         pltpu.VMEM((2, 2, 2, 2, 128), f32),
         pltpu.VMEM((12, 8, 128), f32),
-        pltpu.SemaphoreType.DMA((3,)),
+        pltpu.SemaphoreType.DMA((9,)),
         pltpu.SemaphoreType.DMA((26,)),
         pltpu.SemaphoreType.DMA((26,)),
+        pltpu.SemaphoreType.REGULAR((26,)),
+        pltpu.SemaphoreType.REGULAR,
     ]
     return pl.pallas_call(
         kernel,

time: 24.8 us -> 23.1 us (0.931)
  Pallas kernels: 23.6 us -> 21.9 us
    pallas_call x1, Pallas kernels: 23.6 us -> 21.9 us  [body(): pl.pallas_call(kernel, out_shape=jax.ShapeDtypeStruct(populations.shape,...]
where the time goes in v4:
time: 23.1 us; the launch traced here: 23 us
  Pallas kernels  21.9 us (95%)
  local copies, waits for them, and re-layouts  1.04 us (5%)
    pallas_call x1, Pallas kernels, body(): pl.pallas_call(kernel, out_shape=jax.ShapeDtypeStruct(populations.shape,...  21.9 us
    unnamed x1, local copies, waits for them, and re-layouts  1.04 us

profile of v4, /device:TPU:1, one launch (start us, length us, event | category | flops | bytes accessed | tf_op | source)
XLA Modules:
  0.0 23.0 jit_solution(6425894980737849329)
XLA Ops:
  0.0 21.9 %shard_map.28 = f32[2,19,4,16,128]{4,3,2,1,0:T(8,128)S(1)} custom-call(f32[2,19,4,16,128]{4,3,2,1,0:T(8,128)} %pop.1, s32[4,16,128]{2,1,0:T(8,128)} %solid.1), custom_call_target="tpu_custom_call" | custom-call | tf_op jit(solution)/shard_map/pallas_call | solution.py:510
  21.9 1.0 %copy.4 = f32[2,19,4,16,128]{4,3,2,1,0:T(8,128)} copy(f32[2,19,4,16,128]{4,3,2,1,0:T(8,128)S(1)} %shard_map.28) | data formatting | bytes 2490368

commit v5 on v4

--- a/solution.py
+++ b/solution.py
@@ -97,7 +97,8 @@
         rank = (lambda g: jnp.where(g < 2, g, 5 - g)) if nz == 4 else (lambda g: -g)
         return rank(iz) > rank(lax.rem(iz + dz + nz, nz))
     if dx:
-        return lax.rem(ix, 4) > lax.rem(lax.rem(ix + dx + nx, nx), 4)
+        place = lambda g: jnp.where(lax.rem(g, 4) == 3, 1, 2 * lax.rem(g, 4))
+        return place(ix) > place(lax.rem(ix + dx + nx, nx))
     return None
 
 

time: 23.1 us -> 23 us (level)
  no operation moved by 1% of the time
where the time goes in v5:
time: 23 us; the launch traced here: 22.8 us
  Pallas kernels  21.8 us (95%)
  local copies, waits for them, and re-layouts  1.04 us (5%)
    pallas_call x1, Pallas kernels, body(): pl.pallas_call(kernel, out_shape=jax.ShapeDtypeStruct(populations.shape,...  21.8 us
    unnamed x1, local copies, waits for them, and re-layouts  1.04 us

profile of v5, /device:TPU:1, one launch (start us, length us, event | category | flops | bytes accessed | tf_op | source)
XLA Modules:
  0.0 22.8 jit_solution(14295445666748973023)
XLA Ops:
  0.0 21.8 %shard_map.28 = f32[2,19,4,16,128]{4,3,2,1,0:T(8,128)S(1)} custom-call(f32[2,19,4,16,128]{4,3,2,1,0:T(8,128)} %pop.1, s32[4,16,128]{2,1,0:T(8,128)} %solid.1), custom_call_target="tpu_custom_call" | custom-call | tf_op jit(solution)/shard_map/pallas_call | solution.py:511
  21.8 1.0 %copy.4 = f32[2,19,4,16,128]{4,3,2,1,0:T(8,128)} copy(f32[2,19,4,16,128]{4,3,2,1,0:T(8,128)S(1)} %shard_map.28) | data formatting | bytes 2490368

commit v6 on v5

--- a/solution.py
+++ b/solution.py
@@ -115,7 +115,7 @@
     ix, iy, iz = lax.axis_index("gx"), lax.axis_index("gy"), lax.axis_index("gz")
     nx, ny, nz = lax.axis_size("gx"), lax.axis_size("gy"), lax.axis_size("gz")
     around = (0, 1, -1)
-    groups = [(dx, dz) for dz in (1, -1) for dx in around] + [(1, 0), (-1, 0)]
+    groups = [(dx, dz) for dz in (1, -1) for dx in (1, -1, 0)] + [(1, 0), (-1, 0)]
     leads = {g: ahead(ix, iz, nx, nz, *g) for g in groups}
     told = {g: vouched(ix, iz, nx, nz, *g) for g in groups}
     sends_first = {g: leads[g] & jnp.logical_not(told[g]) for g in groups}

time: 23 us -> 22.8 us (level)
  no operation moved by 1% of the time
where the time goes in v6:
time: 22.8 us; the launch traced here: 22.7 us
  Pallas kernels  21.6 us (95%)
  local copies, waits for them, and re-layouts  1.04 us (5%)
    pallas_call x1, Pallas kernels, body(): pl.pallas_call(kernel, out_shape=jax.ShapeDtypeStruct(populations.shape,...  21.6 us
    unnamed x1, local copies, waits for them, and re-layouts  1.04 us

profile of v6, /device:TPU:1, one launch (start us, length us, event | category | flops | bytes accessed | tf_op | source)
XLA Modules:
  0.0 22.7 jit_solution(3628392409964260685)
XLA Ops:
  0.0 21.6 %shard_map.28 = f32[2,19,4,16,128]{4,3,2,1,0:T(8,128)S(1)} custom-call(f32[2,19,4,16,128]{4,3,2,1,0:T(8,128)} %pop.1, s32[4,16,128]{2,1,0:T(8,128)} %solid.1), custom_call_target="tpu_custom_call" | custom-call | tf_op jit(solution)/shard_map/pallas_call | solution.py:511
  21.6 1.0 %copy.4 = f32[2,19,4,16,128]{4,3,2,1,0:T(8,128)} copy(f32[2,19,4,16,128]{4,3,2,1,0:T(8,128)S(1)} %shard_map.28) | data formatting | bytes 2490368
